TPU v7x, 32 devices: a whole 2x2x4 slice. The times are simulated.
32 devices in a mesh: batch: 2 (over x), col: 4 (over z), row: 4 (over y, core).
Axes of the slice: x: 2, y: 2, z: 4, core: 2. Of those that a mesh axis runs over, the one named last changes fastest.
Arguments:
- images: bfloat16 [32, 512, 512, 3], P('batch', 'row', 'col'), parts along dimension 0
- w_down1: bfloat16 [4, 4, 3, 64], replicated
- b_down1: float32 [64], replicated
- w_conv1: bfloat16 [3, 3, 64, 64], replicated
- b_conv1: float32 [64], replicated
- w_down2: bfloat16 [4, 4, 64, 128], replicated
- b_down2: float32 [128], replicated
- w_conv2: bfloat16 [3, 3, 128, 128], replicated
- b_conv2: float32 [128], replicated
- w_down3: bfloat16 [4, 4, 128, 256], replicated
- b_down3: float32 [256], replicated
- w_conv3: bfloat16 [3, 3, 256, 256], replicated
- b_conv3: float32 [256], replicated
Outputs:
- output: bfloat16 [32, 64, 64, 256], P('batch', 'row', 'col'), parts along dimension 0
There are 2 independent parts. A program takes and returns all parts, laid end to end along the dimension named above; an argument that names none is the same for every part.
All inputs are finite; a program needn't handle non-finite values.
Results may differ from a plain program's by a relative error of at most 0.00425.
Values are sent between devices in bfloat16 or wider.
A program may use at most 1 GiB of HBM per device.

v0:
```python
import jax
import jax.numpy as jnp
from jax import lax
from jax.sharding import PartitionSpec as P


def solution(mesh):
    row_len = mesh.shape['row']
    col_len = mesh.shape['col']

    def add_halo(act_tile, axis_name, edge_dim, axis_len):
        if edge_dim == 1:
            head_edge = act_tile[:, :1]
            tail_edge = act_tile[:, -1:]
        else:
            head_edge = act_tile[:, :, :1]
            tail_edge = act_tile[:, :, -1:]
        if axis_len == 1:
            from_prev = jnp.zeros_like(tail_edge)
            from_next = jnp.zeros_like(head_edge)
        else:
            to_next = [(i, i + 1) for i in range(axis_len - 1)]
            to_prev = [(i + 1, i) for i in range(axis_len - 1)]
            from_prev = lax.ppermute(tail_edge, axis_name, to_next)
            from_next = lax.ppermute(head_edge, axis_name, to_prev)
        return jnp.concatenate([from_prev, act_tile, from_next], axis=edge_dim)

    def conv_relu(act_tile, weight, bias_vec, stride):
        padded = add_halo(add_halo(act_tile, 'row', 1, row_len), 'col', 2, col_len)
        summed = lax.conv_general_dilated(padded, weight, (stride, stride), 'VALID', dimension_numbers=('NHWC', 'HWIO', 'NHWC'), preferred_element_type=jnp.float32)
        return jax.nn.relu(summed + bias_vec).astype(jnp.bfloat16)

    def local_encoder(images, w_down1, b_down1, w_conv1, b_conv1, w_down2, b_down2, w_conv2, b_conv2, w_down3, b_down3, w_conv3, b_conv3):
        params = [(w_down1, b_down1, w_conv1, b_conv1), (w_down2, b_down2, w_conv2, b_conv2), (w_down3, b_down3, w_conv3, b_conv3)]
        act_tile = images
        for w_down, b_down, w_conv, b_conv in params:
            act_tile = conv_relu(act_tile, w_down, b_down, 2)
            act_tile = conv_relu(act_tile, w_conv, b_conv, 1)
        return act_tile

    tile_spec = P('batch', 'row', 'col', None)
    return jax.shard_map(local_encoder, mesh=mesh, in_specs=(tile_spec,) + (P(),) * 12, out_specs=tile_spec, check_vma=False)
```

profile of v0, /device:TPU:1, one launch (start us, length us, event | category | flops | bytes accessed | tf_op | source)
XLA Modules:
  0.0 275.1 jit_solution(13388601290692777635)
XLA Ops:
  0.0 1.1 fusion.84
  1.1 0.1 copy.36
  1.2 1.9 collective-permute-start.1
  3.2 0.1 copy.35
  3.3 4.5 %collective-permute-start = (bf16[16,1,128,3]{0,3,2,1:T(4,128)(2,1)S(1)}, bf16[16,1,128,3]{0,3,2,1:T(4,128)(2,1)S(1)}, u32[]{:S(2)}, u32[]{:S(2)}) collective-permute-start(bf16[16,1,128,3]{0,3,2,1:T(4,128)(2,1)S(1)} %copy.35), channel_id=1, source_target_pairs={{0,1},{1,2},{2,3},{4,5},{5,6},{6,7},{8,9},{9,10},{10,11},{12,13},{... | collective-permute-start | bytes 36872 | tf_op jit(solution)/shard_map/ppermute | solution.py:24
  7.8 16.3 %copy.37 = bf16[16,128,128,3]{0,3,2,1:T(4,128)(2,1)} copy(bf16[16,128,128,3]{2,1,3,0:T(8,128)(2,1)} %param.13) | data formatting | bytes 3145728 | tf_op args[0]
  24.2 1.2 pad_maximum_fusion.17
  25.4 0.1 copy.38
  25.5 3.2 %collective-permute-start.2 = (bf16[16,130,1,3]{1,0,3,2:T(8,128)(2,1)S(1)}, bf16[16,130,1,3]{1,0,3,2:T(8,128)(2,1)S(1)}, u32[]{:S(2)}, u32[]{:S(2)}) collective-permute-start(bf16[16,130,1,3]{1,0,3,2:T(8,128)(2,1)S(1)} %copy.38), channel_id=1, source_target_pairs={{0,4},{4,8},{8,12},{1,5},{5,9},{9,13},{2,6},{6,10},{10,14},{3,7},{... | collective-permute-start | bytes 37448 | tf_op jit(solution)/shard_map/ppermute | solution.py:24
  28.7 0.1 copy.39
  28.9 1.3 collective-permute-start.3
  30.2 0.2 copy.40
  30.4 3.5 %collective-permute-done.3 = bf16[16,130,1,3]{1,0,3,2:T(8,128)(2,1)S(1)} collective-permute-done((bf16[16,130,1,3]{1,0,3,2:T(8,128)(2,1)S(1)}, bf16[16,130,1,3]{1,0,3,2:T(8,128)(2,1)S(1)}, u32[]{:S(2)}, u32[]{:S(2)}) %collective-permute-start.3) | collective-permute-done | bytes 12512 | tf_op jit(solution)/shard_map/ppermute | solution.py:25
  33.9 0.2 copy.41
  34.1 71.7 %maximum_convert_fusion.1 = bf16[16,64,64,64]{3,0,2,1:T(8,128)(2,1)S(1)} fusion(f32[64]{0:T(128)S(1)} %copy-done.9, bf16[16,130,1,3]{0,3,2,1:T(4,128)(2,1)S(1)} %copy.41, bf16[16,1,128,3]{0,3,2,1:T(4,128)(2,1)S(1)} %collective-permute-done.1, bf16[16,128,128,3]{0,3,2,1:T(4,128)(2,1)} %copy.37, bf16[16,1,128,3]{0,3,2,1:T(4,128)(2,1)S(1)} %collective-permute-done, ...), kind=kOutput, calls=%fused_computation.1 | convolution fusion | flops 423348096 | bytes 10017408 | tf_op jit(solution)/shard_map/conv_general_dilated | solution.py:30
  105.8 3.4 %collective-permute-start.4 = (bf16[16,1,64,64]{3,0,2,1:T(8,128)(2,1)S(1)}, bf16[16,1,64,64]{3,0,2,1:T(8,128)(2,1)S(1)}, u32[]{:S(2)}, u32[]{:S(2)}) collective-permute-start(bf16[16,1,64,64]{3,0,2,1:T(8,128)(2,1)S(1)} %get-tuple-element.13), channel_id=1, source_target_pairs={{0,1},{1,2},{2,3},{4,5},{5,6},{6,7},{8,9},{9,10},{10,11},{12,13},{... | collective-permute-start | bytes 393224 | tf_op jit(solution)/shard_map/ppermute | solution.py:24
  109.2 0.0 copy-start.5
  109.2 2.1 collective-permute-start.5
  111.3 1.2 collective-permute-done.4
  112.5 4.6 %collective-permute-done.5 = bf16[16,1,64,64]{3,0,2,1:T(8,128)(2,1)S(1)} collective-permute-done((bf16[16,1,64,64]{3,0,2,1:T(8,128)(2,1)S(1)}, bf16[16,1,64,64]{3,0,2,1:T(8,128)(2,1)S(1)}, u32[]{:S(2)}, u32[]{:S(2)}) %collective-permute-start.5) | collective-permute-done | bytes 131104 | tf_op jit(solution)/shard_map/ppermute | solution.py:25
  117.1 0.1 pad_maximum_fusion.5
  117.2 3.2 %collective-permute-start.6 = (bf16[16,66,1,64]{3,0,2,1:T(8,128)(2,1)S(1)}, bf16[16,66,1,64]{3,0,2,1:T(8,128)(2,1)S(1)}, u32[]{:S(2)}, u32[]{:S(2)}) collective-permute-start(bf16[16,66,1,64]{3,0,2,1:T(8,128)(2,1)S(1)} %get-tuple-element.7), channel_id=1, source_target_pairs={{0,4},{4,8},{8,12},{1,5},{5,9},{9,13},{2,6},{6,10},{10,14},{3,7},{... | collective-permute-start | bytes 405512 | tf_op jit(solution)/shard_map/ppermute | solution.py:24
  120.4 1.5 collective-permute-start.7
  121.9 1.9 collective-permute-done.6
  123.8 3.9 %collective-permute-done.7 = bf16[16,66,1,64]{3,0,2,1:T(8,128)(2,1)S(1)} collective-permute-done((bf16[16,66,1,64]{3,0,2,1:T(8,128)(2,1)S(1)}, bf16[16,66,1,64]{3,0,2,1:T(8,128)(2,1)S(1)}, u32[]{:S(2)}, u32[]{:S(2)}) %collective-permute-start.7) | collective-permute-done | bytes 135200 | tf_op jit(solution)/shard_map/ppermute | solution.py:25
  127.6 33.3 %maximum_convert_fusion = bf16[16,64,64,64]{3,0,2,1:T(8,128)(2,1)} fusion(f32[64]{0:T(128)S(1)} %copy-done.10, bf16[3,3,64,64]{3,2,1,0:T(8,128)(2,1)S(1)} %copy-done.5, bf16[16,66,1,64]{3,0,2,1:T(8,128)(2,1)S(1)} %collective-permute-done.7, bf16[16,1,64,64]{3,0,2,1:T(8,128)(2,1)S(1)} %collective-permute-done.5, ...), kind=kOutput, calls=%fused_computation | convolution fusion | flops 4862263296 | bytes 17383680 | tf_op jit(solution)/shard_map/conv_general_dilated | solution.py:30
  160.9 1.1 fusion.79
  162.0 3.2 %collective-permute-start.8 = (bf16[16,1,64,64]{3,0,2,1:T(8,128)(2,1)S(1)}, bf16[16,1,64,64]{3,0,2,1:T(8,128)(2,1)S(1)}, u32[]{:S(2)}, u32[]{:S(2)}) collective-permute-start(bf16[16,1,64,64]{3,0,2,1:T(8,128)(2,1)S(1)} %get-tuple-element.11), channel_id=1, source_target_pairs={{0,1},{1,2},{2,3},{4,5},{5,6},{6,7},{8,9},{9,10},{10,11},{12,13},{... | collective-permute-start | bytes 393224 | tf_op jit(solution)/shard_map/ppermute | solution.py:24
  165.2 0.0 copy-start.11
  165.2 2.3 collective-permute-start.9
  167.5 0.9 collective-permute-done.8
  168.4 4.8 %collective-permute-done.9 = bf16[16,1,64,64]{3,0,2,1:T(8,128)(2,1)S(1)} collective-permute-done((bf16[16,1,64,64]{3,0,2,1:T(8,128)(2,1)S(1)}, bf16[16,1,64,64]{3,0,2,1:T(8,128)(2,1)S(1)}, u32[]{:S(2)}, u32[]{:S(2)}) %collective-permute-start.9) | collective-permute-done | bytes 131104 | tf_op jit(solution)/shard_map/ppermute | solution.py:25
  173.3 1.2 pad_maximum_fusion.2
  174.4 3.2 %collective-permute-start.10 = (bf16[16,66,1,64]{3,0,2,1:T(8,128)(2,1)S(1)}, bf16[16,66,1,64]{3,0,2,1:T(8,128)(2,1)S(1)}, u32[]{:S(2)}, u32[]{:S(2)}) collective-permute-start(bf16[16,66,1,64]{3,0,2,1:T(8,128)(2,1)S(1)} %get-tuple-element.5), channel_id=1, source_target_pairs={{0,4},{4,8},{8,12},{1,5},{5,9},{9,13},{2,6},{6,10},{10,14},{3,7},{... | collective-permute-start | bytes 405512 | tf_op jit(solution)/shard_map/ppermute | solution.py:24
  177.7 0.0 copy-start.12
  177.7 1.4 collective-permute-start.11
  179.1 1.9 collective-permute-done.10
  181.0 4.0 %collective-permute-done.11 = bf16[16,66,1,64]{3,0,2,1:T(8,128)(2,1)S(1)} collective-permute-done((bf16[16,66,1,64]{3,0,2,1:T(8,128)(2,1)S(1)}, bf16[16,66,1,64]{3,0,2,1:T(8,128)(2,1)S(1)}, u32[]{:S(2)}, u32[]{:S(2)}) %collective-permute-start.11) | collective-permute-done | bytes 135200 | tf_op jit(solution)/shard_map/ppermute | solution.py:25
  185.0 16.3 %maximum_convert_fusion.3 = bf16[16,32,32,128]{3,0,2,1:T(8,128)(2,1)S(1)} fusion(f32[128]{0:T(128)S(1)} %copy-done.11, bf16[4,4,64,128]{3,2,1,0:T(8,128)(2,1)S(1)} %copy-done.4, bf16[16,66,1,64]{3,0,2,1:T(8,128)(2,1)S(1)} %collective-permute-done.11, bf16[16,1,64,64]{3,0,2,1:T(8,128)(2,1)S(1)} %collective-permute-done.9, ...), kind=kOutput, calls=%fused_computation.33 | convolution fusion | flops 4319100928 | bytes 13378048 | tf_op jit(solution)/shard_map/conv_general_dilated | solution.py:30
  201.3 3.2 %collective-permute-start.12 = (bf16[16,1,32,128]{3,0,2,1:T(8,128)(2,1)S(1)}, bf16[16,1,32,128]{3,0,2,1:T(8,128)(2,1)S(1)}, u32[]{:S(2)}, u32[]{:S(2)}) collective-permute-start(bf16[16,1,32,128]{3,0,2,1:T(8,128)(2,1)S(1)} %get-tuple-element.21), channel_id=1, source_target_pairs={{0,1},{1,2},{2,3},{4,5},{5,6},{6,7},{8,9},{9,10},{10,11},{12,13},{... | collective-permute-start | bytes 393224 | tf_op jit(solution)/shard_map/ppermute | solution.py:24
  204.5 1.9 collective-permute-start.13
  206.4 4.3 %collective-permute-done.13 = bf16[16,1,32,128]{3,0,2,1:T(8,128)(2,1)S(1)} collective-permute-done((bf16[16,1,32,128]{3,0,2,1:T(8,128)(2,1)S(1)}, bf16[16,1,32,128]{3,0,2,1:T(8,128)(2,1)S(1)}, u32[]{:S(2)}, u32[]{:S(2)}) %collective-permute-start.13) | collective-permute-done | bytes 131104 | tf_op jit(solution)/shard_map/ppermute | solution.py:25
  210.8 1.6 collective-permute-start.14
  212.5 1.6 collective-permute-start.15
  214.1 0.3 collective-permute-done.14
  214.5 4.0 %collective-permute-done.15 = bf16[16,34,1,128]{3,0,2,1:T(8,128)(2,1)S(1)} collective-permute-done((bf16[16,34,1,128]{3,0,2,1:T(8,128)(2,1)S(1)}, bf16[16,34,1,128]{3,0,2,1:T(8,128)(2,1)S(1)}, u32[]{:S(2)}, u32[]{:S(2)}) %collective-permute-start.15) | collective-permute-done | bytes 139296 | tf_op jit(solution)/shard_map/ppermute | solution.py:25
  218.4 10.2 %maximum_convert_fusion.2 = bf16[16,32,32,128]{3,0,2,1:T(8,128)(2,1)S(1)} fusion(f32[128]{0:T(128)S(1)} %copy-done.12, bf16[3,3,128,128]{3,2,1,0:T(8,128)(2,1)S(1)} %copy-done.3, bf16[16,34,1,128]{3,0,2,1:T(8,128)(2,1)S(1)} %collective-permute-done.15, bf16[16,1,32,128]{3,0,2,1:T(8,128)(2,1)S(1)} %collective-permute-done.13, ...), kind=kOutput, calls=%fused_computation.32 | convolution fusion | flops 4847599616 | bytes 9224704 | tf_op jit(solution)/shard_map/conv_general_dilated | solution.py:30
  228.7 3.2 %collective-permute-start.16 = (bf16[16,1,32,128]{3,0,2,1:T(8,128)(2,1)S(1)}, bf16[16,1,32,128]{3,0,2,1:T(8,128)(2,1)S(1)}, u32[]{:S(2)}, u32[]{:S(2)}) collective-permute-start(bf16[16,1,32,128]{3,0,2,1:T(8,128)(2,1)S(1)} %get-tuple-element.19), channel_id=1, source_target_pairs={{0,1},{1,2},{2,3},{4,5},{5,6},{6,7},{8,9},{9,10},{10,11},{12,13},{... | collective-permute-start | bytes 393224 | tf_op jit(solution)/shard_map/ppermute | solution.py:24
  231.9 1.9 collective-permute-start.17
  233.9 4.3 %collective-permute-done.17 = bf16[16,1,32,128]{3,0,2,1:T(8,128)(2,1)S(1)} collective-permute-done((bf16[16,1,32,128]{3,0,2,1:T(8,128)(2,1)S(1)}, bf16[16,1,32,128]{3,0,2,1:T(8,128)(2,1)S(1)}, u32[]{:S(2)}, u32[]{:S(2)}) %collective-permute-start.17) | collective-permute-done | bytes 131104 | tf_op jit(solution)/shard_map/ppermute | solution.py:25
  238.2 1.6 collective-permute-start.18
  239.9 1.3 collective-permute-start.19
  241.2 0.7 collective-permute-done.18
  241.9 3.8 %collective-permute-done.19 = bf16[16,34,1,128]{3,0,2,1:T(8,128)(2,1)S(1)} collective-permute-done((bf16[16,34,1,128]{3,0,2,1:T(8,128)(2,1)S(1)}, bf16[16,34,1,128]{3,0,2,1:T(8,128)(2,1)S(1)}, u32[]{:S(2)}, u32[]{:S(2)}) %collective-permute-start.19) | collective-permute-done | bytes 139296 | tf_op jit(solution)/shard_map/ppermute | solution.py:25
  245.7 4.9 %maximum_convert_fusion.5 = bf16[16,16,16,256]{3,0,2,1:T(8,128)(2,1)S(1)} fusion(f32[256]{0:T(256)S(1)} %copy-done.7, bf16[4,4,128,256]{3,2,1,0:T(8,128)(2,1)S(1)} %copy-done.2, bf16[16,34,1,128]{3,0,2,1:T(8,128)(2,1)S(1)} %collective-permute-done.19, bf16[16,1,32,128]{3,0,2,1:T(8,128)(2,1)S(1)} %collective-permute-done.17, ...), kind=kOutput, calls=%fused_computation.55 | convolution fusion | flops 4307582976 | bytes 7881728 | tf_op jit(solution)/shard_map/conv_general_dilated | solution.py:30
  250.6 3.2 %collective-permute-start.20 = (bf16[16,1,16,256]{3,0,2,1:T(8,128)(2,1)S(1)}, bf16[16,1,16,256]{3,0,2,1:T(8,128)(2,1)S(1)}, u32[]{:S(2)}, u32[]{:S(2)}) collective-permute-start(bf16[16,1,16,256]{3,0,2,1:T(8,128)(2,1)S(1)} %get-tuple-element.25), channel_id=1, source_target_pairs={{0,1},{1,2},{2,3},{4,5},{5,6},{6,7},{8,9},{9,10},{10,11},{12,13},{... | collective-permute-start | bytes 393224 | tf_op jit(solution)/shard_map/ppermute | solution.py:24
  253.8 1.9 collective-permute-start.21
  255.8 4.3 %collective-permute-done.21 = bf16[16,1,16,256]{3,0,2,1:T(8,128)(2,1)S(1)} collective-permute-done((bf16[16,1,16,256]{3,0,2,1:T(8,128)(2,1)S(1)}, bf16[16,1,16,256]{3,0,2,1:T(8,128)(2,1)S(1)}, u32[]{:S(2)}, u32[]{:S(2)}) %collective-permute-start.21) | collective-permute-done | bytes 131104 | tf_op jit(solution)/shard_map/ppermute | solution.py:25
  260.2 1.6 collective-permute-start.22
  261.8 1.3 collective-permute-start.23
  263.1 0.8 collective-permute-done.22
  263.9 3.8 %collective-permute-done.23 = bf16[16,18,1,256]{3,0,2,1:T(8,128)(2,1)S(1)} collective-permute-done((bf16[16,18,1,256]{3,0,2,1:T(8,128)(2,1)S(1)}, bf16[16,18,1,256]{3,0,2,1:T(8,128)(2,1)S(1)}, u32[]{:S(2)}, u32[]{:S(2)}) %collective-permute-start.23) | collective-permute-done | bytes 147488 | tf_op jit(solution)/shard_map/ppermute | solution.py:25
  267.7 5.4 %maximum_convert_fusion.4 = bf16[16,16,16,256]{3,0,2,1:T(8,128)(2,1)S(1)} fusion(f32[256]{0:T(256)S(1)} %copy-done.8, bf16[3,3,256,256]{3,2,1,0:T(8,128)(2,1)S(1)} %copy-done, bf16[16,18,1,256]{3,0,2,1:T(8,128)(2,1)S(1)} %collective-permute-done.23, bf16[16,1,16,256]{3,0,2,1:T(8,128)(2,1)S(1)} %collective-permute-done.21, ...), kind=kOutput, calls=%fused_computation.54 | convolution fusion | flops 4840292352 | bytes 5932032 | tf_op jit(solution)/shard_map/conv_general_dilated | solution.py:30
  273.1 2.0 copy.43
  (36 shorter events, 0.3 us)
Async XLA Ops:
  0.0 267.7 %copy-start = (bf16[3,3,256,256]{3,2,1,0:T(8,128)(2,1)S(1)}, bf16[3,3,256,256]{3,2,1,0:T(8,128)(2,1)}, u32[]{:S(2)}) copy-start(bf16[3,3,256,256]{3,2,1,0:T(8,128)(2,1)} %param.24) | copy-start | bytes 3538948
  1.2 22.9 %collective-permute-start.1 = (bf16[16,1,128,3]{0,3,2,1:T(4,128)(2,1)S(1)}, bf16[16,1,128,3]{0,3,2,1:T(4,128)(2,1)S(1)}, u32[]{:S(2)}, u32[]{:S(2)}) collective-permute-start(bf16[16,1,128,3]{0,3,2,1:T(4,128)(2,1)S(1)} %copy.36), channel_id=1, source_target_pairs={{1,0},{2,1},{3,2},{5,4},{6,5},{7,6},{9,8},{10,9},{11,10},{13,12},{... | collective-permute-start | bytes 36872 | tf_op jit(solution)/shard_map/ppermute | solution.py:25
  3.3 20.9 %collective-permute-start = (bf16[16,1,128,3]{0,3,2,1:T(4,128)(2,1)S(1)}, bf16[16,1,128,3]{0,3,2,1:T(4,128)(2,1)S(1)}, u32[]{:S(2)}, u32[]{:S(2)}) collective-permute-start(bf16[16,1,128,3]{0,3,2,1:T(4,128)(2,1)S(1)} %copy.35), channel_id=1, source_target_pairs={{0,1},{1,2},{2,3},{4,5},{5,6},{6,7},{8,9},{9,10},{10,11},{12,13},{... | collective-permute-start | bytes 36872 | tf_op jit(solution)/shard_map/ppermute | solution.py:24
  24.2 9.9 %copy-start.6 = (bf16[4,4,3,64]{3,1,2,0:T(4,128)(2,1)S(1)}, bf16[4,4,3,64]{3,1,2,0:T(4,128)(2,1)}, u32[]{:S(2)}) copy-start(bf16[4,4,3,64]{3,1,2,0:T(4,128)(2,1)} %param.14) | copy-start | bytes 18436
  24.2 9.9 %copy-start.9 = (f32[64]{0:T(128)S(1)}, f32[64]{0:T(128)}, u32[]{:S(2)}) copy-start(f32[64]{0:T(128)} %param.15) | copy-start | bytes 772
  25.5 4.6 %collective-permute-start.2 = (bf16[16,130,1,3]{1,0,3,2:T(8,128)(2,1)S(1)}, bf16[16,130,1,3]{1,0,3,2:T(8,128)(2,1)S(1)}, u32[]{:S(2)}, u32[]{:S(2)}) collective-permute-start(bf16[16,130,1,3]{1,0,3,2:T(8,128)(2,1)S(1)} %copy.38), channel_id=1, source_target_pairs={{0,4},{4,8},{8,12},{1,5},{5,9},{9,13},{2,6},{6,10},{10,14},{3,7},{... | collective-permute-start | bytes 37448 | tf_op jit(solution)/shard_map/ppermute | solution.py:24
  28.9 5.0 %collective-permute-start.3 = (bf16[16,130,1,3]{1,0,3,2:T(8,128)(2,1)S(1)}, bf16[16,130,1,3]{1,0,3,2:T(8,128)(2,1)S(1)}, u32[]{:S(2)}, u32[]{:S(2)}) collective-permute-start(bf16[16,130,1,3]{1,0,3,2:T(8,128)(2,1)S(1)} %copy.39), channel_id=1, source_target_pairs={{4,0},{8,4},{12,8},{5,1},{9,5},{13,9},{6,2},{10,6},{14,10},{7,3},{... | collective-permute-start | bytes 37448 | tf_op jit(solution)/shard_map/ppermute | solution.py:25
  105.8 6.7 %collective-permute-start.4 = (bf16[16,1,64,64]{3,0,2,1:T(8,128)(2,1)S(1)}, bf16[16,1,64,64]{3,0,2,1:T(8,128)(2,1)S(1)}, u32[]{:S(2)}, u32[]{:S(2)}) collective-permute-start(bf16[16,1,64,64]{3,0,2,1:T(8,128)(2,1)S(1)} %get-tuple-element.13), channel_id=1, source_target_pairs={{0,1},{1,2},{2,3},{4,5},{5,6},{6,7},{8,9},{9,10},{10,11},{12,13},{... | collective-permute-start | bytes 393224 | tf_op jit(solution)/shard_map/ppermute | solution.py:24
  109.2 18.4 %copy-start.5 = (bf16[3,3,64,64]{3,2,1,0:T(8,128)(2,1)S(1)}, bf16[3,3,64,64]{3,2,1,0:T(8,128)(2,1)}, u32[]{:S(2)}) copy-start(bf16[3,3,64,64]{3,2,1,0:T(8,128)(2,1)} %param.16) | copy-start | bytes 221188
  109.2 18.4 %copy-start.10 = (f32[64]{0:T(128)S(1)}, f32[64]{0:T(128)}, u32[]{:S(2)}) copy-start(f32[64]{0:T(128)} %param.17) | copy-start | bytes 772
  109.2 7.8 %collective-permute-start.5 = (bf16[16,1,64,64]{3,0,2,1:T(8,128)(2,1)S(1)}, bf16[16,1,64,64]{3,0,2,1:T(8,128)(2,1)S(1)}, u32[]{:S(2)}, u32[]{:S(2)}) collective-permute-start(bf16[16,1,64,64]{3,0,2,1:T(8,128)(2,1)S(1)} %get-tuple-element.14), channel_id=1, source_target_pairs={{1,0},{2,1},{3,2},{5,4},{6,5},{7,6},{9,8},{10,9},{11,10},{13,12},{... | collective-permute-start | bytes 393224 | tf_op jit(solution)/shard_map/ppermute | solution.py:25
  117.2 6.6 %collective-permute-start.6 = (bf16[16,66,1,64]{3,0,2,1:T(8,128)(2,1)S(1)}, bf16[16,66,1,64]{3,0,2,1:T(8,128)(2,1)S(1)}, u32[]{:S(2)}, u32[]{:S(2)}) collective-permute-start(bf16[16,66,1,64]{3,0,2,1:T(8,128)(2,1)S(1)} %get-tuple-element.7), channel_id=1, source_target_pairs={{0,4},{4,8},{8,12},{1,5},{5,9},{9,13},{2,6},{6,10},{10,14},{3,7},{... | collective-permute-start | bytes 405512 | tf_op jit(solution)/shard_map/ppermute | solution.py:24
  120.4 7.2 %collective-permute-start.7 = (bf16[16,66,1,64]{3,0,2,1:T(8,128)(2,1)S(1)}, bf16[16,66,1,64]{3,0,2,1:T(8,128)(2,1)S(1)}, u32[]{:S(2)}, u32[]{:S(2)}) collective-permute-start(bf16[16,66,1,64]{3,0,2,1:T(8,128)(2,1)S(1)} %get-tuple-element.8), channel_id=1, source_target_pairs={{4,0},{8,4},{12,8},{5,1},{9,5},{13,9},{6,2},{10,6},{14,10},{7,3},{... | collective-permute-start | bytes 405512 | tf_op jit(solution)/shard_map/ppermute | solution.py:25
  162.0 6.4 %collective-permute-start.8 = (bf16[16,1,64,64]{3,0,2,1:T(8,128)(2,1)S(1)}, bf16[16,1,64,64]{3,0,2,1:T(8,128)(2,1)S(1)}, u32[]{:S(2)}, u32[]{:S(2)}) collective-permute-start(bf16[16,1,64,64]{3,0,2,1:T(8,128)(2,1)S(1)} %get-tuple-element.11), channel_id=1, source_target_pairs={{0,1},{1,2},{2,3},{4,5},{5,6},{6,7},{8,9},{9,10},{10,11},{12,13},{... | collective-permute-start | bytes 393224 | tf_op jit(solution)/shard_map/ppermute | solution.py:24
  165.1 19.9 %copy-start.1 = (bf16[16,64,64,64]{3,0,2,1:T(8,128)(2,1)S(1)}, bf16[16,64,64,64]{3,0,2,1:T(8,128)(2,1)}, u32[]{:S(2)}) copy-start(bf16[16,64,64,64]{3,0,2,1:T(8,128)(2,1)} %maximum_convert_fusion) | copy-start | bytes 25165828
  165.1 19.9 %copy-start.4 = (bf16[4,4,64,128]{3,2,1,0:T(8,128)(2,1)S(1)}, bf16[4,4,64,128]{3,2,1,0:T(8,128)(2,1)}, u32[]{:S(2)}) copy-start(bf16[4,4,64,128]{3,2,1,0:T(8,128)(2,1)} %param.18) | copy-start | bytes 786436
  165.2 19.9 %copy-start.11 = (f32[128]{0:T(128)S(1)}, f32[128]{0:T(128)}, u32[]{:S(2)}) copy-start(f32[128]{0:T(128)} %param.19) | copy-start | bytes 1540
  165.2 8.1 %collective-permute-start.9 = (bf16[16,1,64,64]{3,0,2,1:T(8,128)(2,1)S(1)}, bf16[16,1,64,64]{3,0,2,1:T(8,128)(2,1)S(1)}, u32[]{:S(2)}, u32[]{:S(2)}) collective-permute-start(bf16[16,1,64,64]{3,0,2,1:T(8,128)(2,1)S(1)} %get-tuple-element.12), channel_id=1, source_target_pairs={{1,0},{2,1},{3,2},{5,4},{6,5},{7,6},{9,8},{10,9},{11,10},{13,12},{... | collective-permute-start | bytes 393224 | tf_op jit(solution)/shard_map/ppermute | solution.py:25
  174.4 6.6 %collective-permute-start.10 = (bf16[16,66,1,64]{3,0,2,1:T(8,128)(2,1)S(1)}, bf16[16,66,1,64]{3,0,2,1:T(8,128)(2,1)S(1)}, u32[]{:S(2)}, u32[]{:S(2)}) collective-permute-start(bf16[16,66,1,64]{3,0,2,1:T(8,128)(2,1)S(1)} %get-tuple-element.5), channel_id=1, source_target_pairs={{0,4},{4,8},{8,12},{1,5},{5,9},{9,13},{2,6},{6,10},{10,14},{3,7},{... | collective-permute-start | bytes 405512 | tf_op jit(solution)/shard_map/ppermute | solution.py:24
  177.7 40.8 %copy-start.3 = (bf16[3,3,128,128]{3,2,1,0:T(8,128)(2,1)S(1)}, bf16[3,3,128,128]{3,2,1,0:T(8,128)(2,1)}, u32[]{:S(2)}) copy-start(bf16[3,3,128,128]{3,2,1,0:T(8,128)(2,1)} %param.20) | copy-start | bytes 884740
  177.7 40.8 %copy-start.12 = (f32[128]{0:T(128)S(1)}, f32[128]{0:T(128)}, u32[]{:S(2)}) copy-start(f32[128]{0:T(128)} %param.21) | copy-start | bytes 1540
  177.7 7.3 %collective-permute-start.11 = (bf16[16,66,1,64]{3,0,2,1:T(8,128)(2,1)S(1)}, bf16[16,66,1,64]{3,0,2,1:T(8,128)(2,1)S(1)}, u32[]{:S(2)}, u32[]{:S(2)}) collective-permute-start(bf16[16,66,1,64]{3,0,2,1:T(8,128)(2,1)S(1)} %get-tuple-element.6), channel_id=1, source_target_pairs={{4,0},{8,4},{12,8},{5,1},{9,5},{13,9},{6,2},{10,6},{14,10},{7,3},{... | collective-permute-start | bytes 405512 | tf_op jit(solution)/shard_map/ppermute | solution.py:25
  201.3 5.1 %collective-permute-start.12 = (bf16[16,1,32,128]{3,0,2,1:T(8,128)(2,1)S(1)}, bf16[16,1,32,128]{3,0,2,1:T(8,128)(2,1)S(1)}, u32[]{:S(2)}, u32[]{:S(2)}) collective-permute-start(bf16[16,1,32,128]{3,0,2,1:T(8,128)(2,1)S(1)} %get-tuple-element.21), channel_id=1, source_target_pairs={{0,1},{1,2},{2,3},{4,5},{5,6},{6,7},{8,9},{9,10},{10,11},{12,13},{... | collective-permute-start | bytes 393224 | tf_op jit(solution)/shard_map/ppermute | solution.py:24
  204.5 6.3 %collective-permute-start.13 = (bf16[16,1,32,128]{3,0,2,1:T(8,128)(2,1)S(1)}, bf16[16,1,32,128]{3,0,2,1:T(8,128)(2,1)S(1)}, u32[]{:S(2)}, u32[]{:S(2)}) collective-permute-start(bf16[16,1,32,128]{3,0,2,1:T(8,128)(2,1)S(1)} %get-tuple-element.22), channel_id=1, source_target_pairs={{1,0},{2,1},{3,2},{5,4},{6,5},{7,6},{9,8},{10,9},{11,10},{13,12},{... | collective-permute-start | bytes 393224 | tf_op jit(solution)/shard_map/ppermute | solution.py:25
  210.8 3.6 %collective-permute-start.14 = (bf16[16,34,1,128]{3,0,2,1:T(8,128)(2,1)S(1)}, bf16[16,34,1,128]{3,0,2,1:T(8,128)(2,1)S(1)}, u32[]{:S(2)}, u32[]{:S(2)}) collective-permute-start(bf16[16,34,1,128]{3,0,2,1:T(8,128)(2,1)S(1)} %get-tuple-element.17), channel_id=1, source_target_pairs={{0,4},{4,8},{8,12},{1,5},{5,9},{9,13},{2,6},{6,10},{10,14},{3,7},{... | collective-permute-start | bytes 417800 | tf_op jit(solution)/shard_map/ppermute | solution.py:24
  212.5 33.2 %copy-start.2 = (bf16[4,4,128,256]{3,2,1,0:T(8,128)(2,1)S(1)}, bf16[4,4,128,256]{3,2,1,0:T(8,128)(2,1)}, u32[]{:S(2)}) copy-start(bf16[4,4,128,256]{3,2,1,0:T(8,128)(2,1)} %param.22) | copy-start | bytes 3145732
  212.5 33.2 %copy-start.7 = (f32[256]{0:T(256)S(1)}, f32[256]{0:T(256)}, u32[]{:S(2)}) copy-start(f32[256]{0:T(256)} %param.23) | copy-start | bytes 3076
  212.5 5.9 %collective-permute-start.15 = (bf16[16,34,1,128]{3,0,2,1:T(8,128)(2,1)S(1)}, bf16[16,34,1,128]{3,0,2,1:T(8,128)(2,1)S(1)}, u32[]{:S(2)}, u32[]{:S(2)}) collective-permute-start(bf16[16,34,1,128]{3,0,2,1:T(8,128)(2,1)S(1)} %get-tuple-element.18), channel_id=1, source_target_pairs={{4,0},{8,4},{12,8},{5,1},{9,5},{13,9},{6,2},{10,6},{14,10},{7,3},{... | collective-permute-start | bytes 417800 | tf_op jit(solution)/shard_map/ppermute | solution.py:25
  228.7 5.2 %collective-permute-start.16 = (bf16[16,1,32,128]{3,0,2,1:T(8,128)(2,1)S(1)}, bf16[16,1,32,128]{3,0,2,1:T(8,128)(2,1)S(1)}, u32[]{:S(2)}, u32[]{:S(2)}) collective-permute-start(bf16[16,1,32,128]{3,0,2,1:T(8,128)(2,1)S(1)} %get-tuple-element.19), channel_id=1, source_target_pairs={{0,1},{1,2},{2,3},{4,5},{5,6},{6,7},{8,9},{9,10},{10,11},{12,13},{... | collective-permute-start | bytes 393224 | tf_op jit(solution)/shard_map/ppermute | solution.py:24
  231.9 6.3 %collective-permute-start.17 = (bf16[16,1,32,128]{3,0,2,1:T(8,128)(2,1)S(1)}, bf16[16,1,32,128]{3,0,2,1:T(8,128)(2,1)S(1)}, u32[]{:S(2)}, u32[]{:S(2)}) collective-permute-start(bf16[16,1,32,128]{3,0,2,1:T(8,128)(2,1)S(1)} %get-tuple-element.20), channel_id=1, source_target_pairs={{1,0},{2,1},{3,2},{5,4},{6,5},{7,6},{9,8},{10,9},{11,10},{13,12},{... | collective-permute-start | bytes 393224 | tf_op jit(solution)/shard_map/ppermute | solution.py:25
  238.2 3.6 %collective-permute-start.18 = (bf16[16,34,1,128]{3,0,2,1:T(8,128)(2,1)S(1)}, bf16[16,34,1,128]{3,0,2,1:T(8,128)(2,1)S(1)}, u32[]{:S(2)}, u32[]{:S(2)}) collective-permute-start(bf16[16,34,1,128]{3,0,2,1:T(8,128)(2,1)S(1)} %get-tuple-element.15), channel_id=1, source_target_pairs={{0,4},{4,8},{8,12},{1,5},{5,9},{9,13},{2,6},{6,10},{10,14},{3,7},{... | collective-permute-start | bytes 417800 | tf_op jit(solution)/shard_map/ppermute | solution.py:24
  239.9 27.8 %copy-start.8 = (f32[256]{0:T(256)S(1)}, f32[256]{0:T(256)}, u32[]{:S(2)}) copy-start(f32[256]{0:T(256)} %param.25) | copy-start | bytes 3076
  239.9 5.8 %collective-permute-start.19 = (bf16[16,34,1,128]{3,0,2,1:T(8,128)(2,1)S(1)}, bf16[16,34,1,128]{3,0,2,1:T(8,128)(2,1)S(1)}, u32[]{:S(2)}, u32[]{:S(2)}) collective-permute-start(bf16[16,34,1,128]{3,0,2,1:T(8,128)(2,1)S(1)} %get-tuple-element.16), channel_id=1, source_target_pairs={{4,0},{8,4},{12,8},{5,1},{9,5},{13,9},{6,2},{10,6},{14,10},{7,3},{... | collective-permute-start | bytes 417800 | tf_op jit(solution)/shard_map/ppermute | solution.py:25
  250.6 5.2 %collective-permute-start.20 = (bf16[16,1,16,256]{3,0,2,1:T(8,128)(2,1)S(1)}, bf16[16,1,16,256]{3,0,2,1:T(8,128)(2,1)S(1)}, u32[]{:S(2)}, u32[]{:S(2)}) collective-permute-start(bf16[16,1,16,256]{3,0,2,1:T(8,128)(2,1)S(1)} %get-tuple-element.25), channel_id=1, source_target_pairs={{0,1},{1,2},{2,3},{4,5},{5,6},{6,7},{8,9},{9,10},{10,11},{12,13},{... | collective-permute-start | bytes 393224 | tf_op jit(solution)/shard_map/ppermute | solution.py:24
  253.8 6.3 %collective-permute-start.21 = (bf16[16,1,16,256]{3,0,2,1:T(8,128)(2,1)S(1)}, bf16[16,1,16,256]{3,0,2,1:T(8,128)(2,1)S(1)}, u32[]{:S(2)}, u32[]{:S(2)}) collective-permute-start(bf16[16,1,16,256]{3,0,2,1:T(8,128)(2,1)S(1)} %get-tuple-element.26), channel_id=1, source_target_pairs={{1,0},{2,1},{3,2},{5,4},{6,5},{7,6},{9,8},{10,9},{11,10},{13,12},{... | collective-permute-start | bytes 393224 | tf_op jit(solution)/shard_map/ppermute | solution.py:25
  260.2 3.7 %collective-permute-start.22 = (bf16[16,18,1,256]{3,0,2,1:T(8,128)(2,1)S(1)}, bf16[16,18,1,256]{3,0,2,1:T(8,128)(2,1)S(1)}, u32[]{:S(2)}, u32[]{:S(2)}) collective-permute-start(bf16[16,18,1,256]{3,0,2,1:T(8,128)(2,1)S(1)} %get-tuple-element.23), channel_id=1, source_target_pairs={{0,4},{4,8},{8,12},{1,5},{5,9},{9,13},{2,6},{6,10},{10,14},{3,7},{... | collective-permute-start | bytes 442376 | tf_op jit(solution)/shard_map/ppermute | solution.py:24
  261.8 5.9 %collective-permute-start.23 = (bf16[16,18,1,256]{3,0,2,1:T(8,128)(2,1)S(1)}, bf16[16,18,1,256]{3,0,2,1:T(8,128)(2,1)S(1)}, u32[]{:S(2)}, u32[]{:S(2)}) collective-permute-start(bf16[16,18,1,256]{3,0,2,1:T(8,128)(2,1)S(1)} %get-tuple-element.24), channel_id=1, source_target_pairs={{4,0},{8,4},{12,8},{5,1},{9,5},{13,9},{6,2},{10,6},{14,10},{7,3},{... | collective-permute-start | bytes 442376 | tf_op jit(solution)/shard_map/ppermute | solution.py:25
where the time goes:
time: 277 us; the launch traced here: 275 us
  matrix products  142 us (51%)
  starting transfers between devices  55.7 us (20%)
  waiting for transfers between devices  53.1 us (19%)
  local copies, waits for them, and re-layouts  21.5 us (8%)
    conv_general_dilated x6, matrix products, conv_relu(): lax.conv_general_dilated(padded, weight, (stride, stride), 'VALID', dimen...  142 us
    ppermute x12, waiting for transfers between devices, add_halo(): from_next = lax.ppermute(head_edge, axis_name, to_prev)  45.4 us
    ppermute x12, starting transfers between devices, add_halo(): from_prev = lax.ppermute(tail_edge, axis_name, to_next)  35.2 us
    ppermute x12, starting transfers between devices, add_halo(): from_next = lax.ppermute(head_edge, axis_name, to_prev)  20.5 us
    unnamed x27, local copies, waits for them, and re-layouts  16.4 us
    ppermute x12, waiting for transfers between devices, add_halo(): from_prev = lax.ppermute(tail_edge, axis_name, to_next)  7.67 us
  transfers between devices with their start and end apart: 24, of which 18 were waited for; matrix products, arithmetic and copies ran while one was open for 6% of the time, Pallas kernels for 0%

commit v1 on v0

v1 whole, which is shorter than its diff:
```python
import functools

import jax
import jax.numpy as jnp
from jax import lax
from jax.experimental import pallas as pl
from jax.experimental.pallas import tpu as pltpu
from jax.sharding import PartitionSpec as P

MESH = pl.DeviceIdType.MESH
F32 = jnp.float32
BF16 = jnp.bfloat16


def body(rows, cols, x_ref, wd1, bd1, wc1, bc1, wd2, bd2, wc2, bc2, wd3, bd3, wc3, bc3, out_ref,
         top, bot, tt, send_l, send_r, recv_l, recv_r, y1, z1, y2, z2, y3, ssem, rsem):
    r = lax.axis_index('row')
    c = lax.axis_index('col')
    has_up, has_dn = r > 0, r < rows - 1
    has_lf, has_rt = c > 0, c < cols - 1

    neighbours = []
    for dr in (-1, 0, 1):
        for dc in (-1, 0, 1):
            if dr == 0 and dc == 0:
                continue
            there = None
            if dr:
                there = has_up if dr < 0 else has_dn
            if dc:
                side = has_lf if dc < 0 else has_rt
                there = side if there is None else jnp.logical_and(there, side)
            neighbours.append((dr, dc, there))

    def device(dr, dc):
        return {'row': r + dr, 'col': c + dc}

    barrier = pltpu.get_barrier_semaphore()
    for dr, dc, there in neighbours:
        @pl.when(there)
        def _():
            pl.semaphore_signal(barrier, inc=1, device_id=device(dr, dc), device_id_type=MESH)
    n_r = has_up.astype(jnp.int32) + has_dn.astype(jnp.int32)
    n_c = has_lf.astype(jnp.int32) + has_rt.astype(jnp.int32)
    pl.semaphore_wait(barrier, (n_r + 1) * (n_c + 1) - 1)

    def remote(src, dst, k, dr, dc):
        return pltpu.make_async_remote_copy(src_ref=src, dst_ref=dst, send_sem=ssem.at[k], recv_sem=rsem.at[k],
                                            device_id=device(dr, dc), device_id_type=MESH)

    to_dn = remote(x_ref.at[:, 112:128], top, 0, 1, 0)
    to_up = remote(x_ref.at[:, 0:16], bot, 1, -1, 0)

    @pl.when(has_dn)
    def _():
        to_dn.start()

    @pl.when(has_up)
    def _():
        to_up.start()

    @pl.when(jnp.logical_not(has_up))
    def _():
        top[...] = jnp.zeros_like(top)

    @pl.when(jnp.logical_not(has_dn))
    def _():
        bot[...] = jnp.zeros_like(bot)

    def put(cu, g, stack):
        t = jnp.transpose(stack.astype(F32))
        lanes = slice(g * 128, g * 128 + 128)
        tt[cu, 13:141, lanes] = t
        send_l[cu, :, lanes] = t[0:16].astype(BF16)
        send_r[cu, :, lanes] = t[112:128].astype(BF16)

    def inner(ch, _):
        for u in range(4):
            for g in (1, 2, 3):
                h0 = 32 * g + u - 13
                pieces = [x_ref[ch, h0 + 4 * k] for k in range(8)]
                put(ch * 4 + u, g, jnp.concatenate(pieces, axis=0))
        return 0

    lax.fori_loop(0, 3, inner, 0)

    @pl.when(has_up)
    def _():
        to_up.wait_send()
        remote(x_ref.at[:, 112:128], top, 0, 1, 0).wait_recv()

    @pl.when(has_dn)
    def _():
        to_dn.wait_send()
        remote(x_ref.at[:, 0:16], bot, 1, -1, 0).wait_recv()

    def outer(ch, _):
        for u in range(4):
            for g in (0, 4):
                pieces = []
                for k in range(8):
                    h = 32 * g + u - 13 + 4 * k
                    if h < 0:
                        pieces.append(top[ch, h + 16])
                    elif h < 128:
                        pieces.append(x_ref[ch, h])
                    elif h < 144:
                        pieces.append(bot[ch, h - 128])
                    else:
                        pieces.append(jnp.zeros((16, 128), BF16))
                put(ch * 4 + u, g, jnp.concatenate(pieces, axis=0))
        return 0

    lax.fori_loop(0, 3, outer, 0)

    to_lf = remote(send_l, recv_r, 2, 0, -1)
    to_rt = remote(send_r, recv_l, 3, 0, 1)

    @pl.when(has_lf)
    def _():
        to_lf.start()

    @pl.when(has_rt)
    def _():
        to_rt.start()

    def dots(pairs):
        acc = None
        for lhs, w in pairs:
            d = jnp.dot(lhs, w, preferred_element_type=F32)
            acc = d if acc is None else acc + d
        return acc

    def finish(acc, bias, shape):
        return jnp.maximum(acc + bias[...], 0.0).astype(BF16).reshape(shape)

    def down1(k, _):
        win = tt[:, pl.ds(pl.multiple_of(8 * k, 8), 16), :]
        for e in range(2):
            xt = jnp.transpose(win[:, 4 * e:4 * e + 8].reshape(96, 640))
            xb = jnp.concatenate([xt.astype(BF16), jnp.zeros((640, 32), BF16)], axis=1)
            lhs = jnp.concatenate([xb[0:608], xb[16:624]], axis=1)
            y1[2 * k + e] = finish(dots([(lhs, wd1[...])]), bd1, (38, 16, 256))
        return 0

    lax.fori_loop(2, 17, down1, 0)

    @pl.when(has_lf)
    def _():
        to_lf.wait_send()
        to_rt.wait_recv()

    @pl.when(has_rt)
    def _():
        to_rt.wait_send()
        to_lf.wait_recv()

    @pl.when(jnp.logical_not(has_lf))
    def _():
        recv_l[...] = jnp.zeros_like(recv_l)

    @pl.when(jnp.logical_not(has_rt))
    def _():
        recv_r[...] = jnp.zeros_like(recv_r)

    tt[:, 0:13, :] = recv_l[...].astype(F32)[:, 3:16]
    tt[:, 141:157, :] = recv_r[...].astype(F32)
    lax.fori_loop(0, 2, down1, 0)
    lax.fori_loop(17, 19, down1, 0)

    def clear(ref, there, index):
        @pl.when(jnp.logical_not(there))
        def _():
            ref[index] = jnp.zeros_like(ref[index])

    every = slice(None)
    clear(y1, has_up, (every, slice(0, 3)))
    clear(y1, has_dn, (every, slice(35, 38)))
    clear(y1, has_lf, (slice(0, 3),))
    clear(y1, has_rt, (slice(35, 38),))

    def conv1(b, _):
        pairs = [(y1[b + dw, dh:dh + 37].reshape(592, 256), wc1[dw, dh]) for dw in range(2) for dh in range(2)]
        z1[b] = finish(dots(pairs), bc1, (37, 16, 256))
        return 0

    lax.fori_loop(0, 37, conv1, 0)
    clear(z1, has_up, (every, slice(0, 2)))
    clear(z1, has_up, (every, slice(2, 3), every, slice(0, 128)))
    clear(z1, has_dn, (every, slice(35, 37)))
    clear(z1, has_dn, (every, slice(34, 35), every, slice(128, 256)))
    clear(z1, has_lf, (slice(0, 2),))
    clear(z1, has_rt, (slice(35, 37),))
    for half in (0, 128):
        clear(z1, has_lf, (slice(2, 3), every, every, slice(half, half + 64)))
        clear(z1, has_rt, (slice(34, 35), every, every, slice(half + 64, half + 128)))

    def down2(p, _):
        pairs = [(z1[2 * p + dw, dh:dh + 36].reshape(576, 256), wd2[dw, dh]) for dw in range(3) for dh in range(2)]
        y2[p] = finish(dots(pairs), bd2, (36, 16, 256))
        return 0

    lax.fori_loop(0, 18, down2, 0)
    clear(y2, has_up, (every, slice(0, 2)))
    clear(y2, has_dn, (every, slice(34, 36)))
    clear(y2, has_lf, (slice(0, 1),))
    clear(y2, has_rt, (slice(17, 18),))

    def conv2(q, _):
        pairs = [(y2[q + dw, dh:dh + 34].reshape(544, 256), wc2[dw, dh]) for dw in range(2) for dh in range(3)]
        z2[q] = finish(dots(pairs), bc2, (34, 16, 256))
        return 0

    lax.fori_loop(0, 17, conv2, 0)
    clear(z2, has_up, (every, slice(0, 1)))
    clear(z2, has_dn, (every, slice(33, 34)))
    clear(z2, has_lf, (slice(0, 1), every, every, slice(0, 128)))
    clear(z2, has_rt, (slice(16, 17), every, every, slice(128, 256)))

    def down3(k, _):
        pairs = []
        for dw in range(2):
            for dh in range(4):
                lhs = [z2[2 * k + e + dw, dh + 2 * i] for e in range(2) for i in range(16)]
                pairs.append((jnp.concatenate(lhs, axis=0), wd3[dw, dh]))
        y3[pl.ds(2 * k + 1, 2), 1:17] = finish(dots(pairs), bd3, (2, 16, 16, 256))
        return 0

    lax.fori_loop(0, 8, down3, 0)

    def edge(d):
        return slice(1, 17) if d == 0 else (slice(16, 17) if d > 0 else slice(1, 2))

    def place(d):
        return slice(1, 17) if d == 0 else (slice(0, 1) if d > 0 else slice(17, 18))

    copies = []
    for k, (dr, dc, there) in enumerate(neighbours):
        copies.append(remote(y3.at[edge(dc), edge(dr)], y3.at[place(dc), place(dr)], 4 + k, dr, dc))

        @pl.when(there)
        def _():
            copies[k].start()
    clear(y3, has_up, (every, slice(0, 1)))
    clear(y3, has_dn, (every, slice(17, 18)))
    clear(y3, has_lf, (slice(0, 1),))
    clear(y3, has_rt, (slice(17, 18),))
    for k, (dr, dc, there) in enumerate(neighbours):
        @pl.when(there)
        def _():
            copies[k].wait_send()
            copies[7 - k].wait_recv()

    def conv3(k, _):
        pairs = []
        for dw in range(3):
            for dh in range(3):
                lhs = y3[pl.ds(2 * k + dw, 2), dh:dh + 16].reshape(512, 256)
                pairs.append((lhs, wc3[dh, dw]))
        out_ref[pl.ds(2 * k, 2)] = finish(dots(pairs), bc3, (2, 16, 16, 256))
        return 0

    lax.fori_loop(0, 8, conv3, 0)


def taps(w, axis, e, step, size):
    pads = [(0, 0)] * w.ndim
    pads[axis] = (step * e, size - w.shape[axis] - step * e)
    return jnp.pad(w, pads)


def solution(mesh):
    rows, cols = mesh.shape['row'], mesh.shape['col']

    def local(images, w_down1, b_down1, w_conv1, b_conv1, w_down2, b_down2, w_conv2, b_conv2, w_down3, b_down3, w_conv3, b_conv3):
        x = jnp.transpose(images, (3, 1, 0, 2))
        w = jnp.concatenate([taps(taps(w_down1, 0, eh, 2, 8), 1, ew, 2, 8) for eh in range(2) for ew in range(2)], axis=3)
        w = w.reshape(2, 4, 8, 3, 256).transpose(0, 3, 1, 2, 4).reshape(2, 96, 256)
        wd1 = jnp.pad(w, ((0, 0), (0, 32), (0, 0))).reshape(256, 256)
        w = jnp.concatenate([taps(taps(w_conv1, 0, eh, 1, 4), 1, ew, 1, 4) for eh in range(2) for ew in range(2)], axis=3)
        wc1 = w.reshape(2, 2, 2, 2, 64, 256).transpose(2, 0, 1, 3, 4, 5).reshape(2, 2, 256, 256)
        w = jnp.concatenate([taps(w_down2, 1, ew, 2, 6) for ew in range(2)], axis=3)
        wd2 = w.reshape(2, 2, 3, 2, 64, 256).transpose(2, 0, 1, 3, 4, 5).reshape(3, 2, 256, 256)
        w = jnp.concatenate([taps(w_conv2, 1, ew, 1, 4) for ew in range(2)], axis=3)
        wc2 = w.reshape(3, 2, 2, 128, 256).transpose(1, 0, 2, 3, 4).reshape(2, 3, 256, 256)
        wd3 = w_down3.reshape(4, 2, 2, 128, 256).transpose(1, 0, 2, 3, 4).reshape(2, 4, 256, 256)

        def bias(b, times):
            return jnp.tile(b, times).reshape(1, 256)

        vmem = pl.BlockSpec(memory_space=pltpu.VMEM)
        out = pl.pallas_call(
            functools.partial(body, rows, cols),
            out_shape=jax.ShapeDtypeStruct((16, 16, 16, 256), BF16),
            in_specs=[vmem] * 13,
            out_specs=vmem,
            scratch_shapes=[
                pltpu.VMEM((3, 16, 16, 128), BF16),
                pltpu.VMEM((3, 16, 16, 128), BF16),
                pltpu.VMEM((12, 160, 640), F32),
                pltpu.VMEM((12, 16, 640), BF16),
                pltpu.VMEM((12, 16, 640), BF16),
                pltpu.VMEM((12, 16, 640), BF16),
                pltpu.VMEM((12, 16, 640), BF16),
                pltpu.VMEM((38, 38, 16, 256), BF16),
                pltpu.VMEM((37, 37, 16, 256), BF16),
                pltpu.VMEM((18, 36, 16, 256), BF16),
                pltpu.VMEM((17, 34, 16, 256), BF16),
                pltpu.VMEM((18, 18, 16, 256), BF16),
                pltpu.SemaphoreType.DMA((12,)),
                pltpu.SemaphoreType.DMA((12,)),
            ],
            compiler_params=pltpu.CompilerParams(collective_id=0, has_side_effects=True, vmem_limit_bytes=66_000_000),
            name='encoder',
        )(x, wd1, bias(b_down1, 4), wc1, bias(b_conv1, 4), wd2, bias(b_down2, 2), wc2, bias(b_conv2, 2),
          wd3, bias(b_down3, 1), w_conv3, bias(b_conv3, 1))
        return jnp.transpose(out, (2, 1, 0, 3))

    tile_spec = P('batch', 'row', 'col', None)
    return jax.shard_map(local, mesh=mesh, in_specs=(tile_spec,) + (P(),) * 12, out_specs=tile_spec, check_vma=False)
```

time: 277 us -> 94.6 us (0.34)
  matrix products: 142 us -> 0 us
  Pallas kernels: 0 us -> 75.6 us
  starting transfers between devices: 55.7 us -> 0 us
  waiting for transfers between devices: 53.1 us -> 0 us
  local copies, waits for them, and re-layouts: 21.5 us -> 18.1 us
    conv_general_dilated x6 -> x0, matrix products: 142 us -> none  [conv_relu(): lax.conv_general_dilated(padded, weight, (stride, stride), 'VALID', dimen...]
    pallas_call x0 -> x1, Pallas kernels: none -> 75.6 us  [local(): pl.pallas_call(functools.partial(body, rows, cols), out_shape=jax.ShapeDt...]
    ppermute x24 -> x0, starting transfers between devices: 55.7 us -> none  [the longest x12 35.2 us: add_halo(): from_prev = lax.ppermute(tail_edge, axis_name, to_next)]
    ppermute x24 -> x0, waiting for transfers between devices: 53.1 us -> none  [the longest x12 45.4 us: add_halo(): from_next = lax.ppermute(head_edge, axis_name, to_prev)]
    unnamed x27 -> x9, local copies, waits for them, and re-layouts: 16.4 us -> 2.63 us
    another operation x0 -> x6, local copies, waits for them, and re-layouts: none -> 5.04 us  [bias(): return jnp.tile(b, times).reshape(1, 256)]
    transpose x0 -> x2, local copies, waits for them, and re-layouts: none -> 4.09 us  [the longest x1 4.08 us: local(): return jnp.transpose(out, (2, 1, 0, 3))]
    reshape x0 -> x4, local copies, waits for them, and re-layouts: none -> 3.82 us  [the longest x1 1.06 us: local(): w_down3.reshape(4, 2, 2, 128, 256).transpose(1, 0, 2, 3, 4)]
  transfers between devices with their start and end apart: 24 -> 0, of which waited for: 18 -> 0; matrix products, arithmetic and copies ran while one was open for 6% -> 0% of each run, Pallas kernels for 0% -> 0%
where the time goes in v1:
time: 94.6 us; the launch traced here: 94.3 us
  Pallas kernels  75.6 us (80%)
  local copies, waits for them, and re-layouts  18.1 us (19%)
    pallas_call x1, Pallas kernels, local(): pl.pallas_call(functools.partial(body, rows, cols), out_shape=jax.ShapeDt...  75.6 us
    another operation x6, local copies, waits for them, and re-layouts, bias(): return jnp.tile(b, times).reshape(1, 256)  5.04 us
    transpose x1, local copies, waits for them, and re-layouts, local(): return jnp.transpose(out, (2, 1, 0, 3))  4.08 us
    unnamed x9, local copies, waits for them, and re-layouts  2.63 us

profile of v1, /device:TPU:1, one launch (start us, length us, event | category | flops | bytes accessed | tf_op | source)
XLA Modules:
  0.0 94.3 jit_solution(1932569754406508934)
XLA Ops:
  0.0 1.2 %tile.14 = f32[2,128]{1,0:T(2,128)} broadcast(f32[128]{0:T(128)} %param.19), dimensions={1} | broadcast | bytes 1536 | tf_op jit(solution)/shard_map/tile | solution.py:289
  1.2 1.2 %tile.15 = f32[2,128]{1,0:T(2,128)} broadcast(f32[128]{0:T(128)} %param.21), dimensions={1} | broadcast | bytes 1536 | tf_op jit(solution)/shard_map/tile | solution.py:289
  2.5 0.7 tile.12
  3.1 0.6 reshape_tile.12.bd1
  3.7 0.7 tile.13
  4.4 0.6 reshape_tile.13.bc1
  5.0 0.0 copy-start.3
  5.0 0.8 fusion.25
  5.8 0.1 fusion.22
  6.0 0.7 pad.74
  6.6 1.1 %fusion.24 = (bf16[4,3,64,64]{3,2,1,0:T(8,128)(2,1)S(1)}, bf16[4,3,64,64]{3,2,1,0:T(8,128)(2,1)S(1)}) fusion(bf16[3,3,64,64]{3,2,1,0:T(8,128)(2,1)} %param.16), kind=kLoop, calls=%fused_computation.41 | loop fusion | bytes 270336 | tf_op jit(solution)/shard_map/jit(_pad)/pad | solution.py:269
  7.7 0.3 fusion.13
  8.0 0.9 copy.16
  8.9 0.0 copy-start.2
  8.9 0.0 copy-done.3
  8.9 0.1 fusion.11
  9.0 1.0 %copy.17 = bf16[2,2,3,2,64,256]{5,4,3,1,0,2:T(8,128)(2,1)} copy(bf16[2,2,3,2,64,256]{5,4,3,2,1,0:T(8,128)(2,1)S(1)} %bitcast.34) | data formatting | bytes 1572864 | tf_op jit(solution)/shard_map/reshape | solution.py:283
  9.9 0.0 copy-start.1
  9.9 0.0 copy-done.2
  9.9 0.1 fusion.10
  10.0 0.0 copy-start
  10.0 1.0 %copy.18 = bf16[3,2,2,128,256]{4,3,2,0,1:T(8,128)(2,1)} copy(bf16[3,2,2,128,256]{4,3,2,1,0:T(8,128)(2,1)S(1)} %bitcast.35) | data formatting | bytes 1572864 | tf_op jit(solution)/shard_map/reshape | solution.py:285
  11.0 0.5 copy-done.1
  11.4 1.1 %copy.19 = bf16[4,2,2,128,256]{4,3,2,0,1:T(8,128)(2,1)} copy(bf16[4,2,2,128,256]{4,3,2,1,0:T(8,128)(2,1)S(1)} %bitcast.38) | data formatting | bytes 2097152 | tf_op jit(solution)/shard_map/reshape | solution.py:286
  12.5 0.0 copy-done
  12.5 2.2 %copy.22 = bf16[16,128,128,3]{2,0,1,3:T(8,128)(2,1)} copy(bf16[16,128,128,3]{2,1,3,0:T(8,128)(2,1)S(1)} %copy-done) | data formatting | bytes 3145728 | tf_op args[0]
  14.6 75.6 %encoder.1 = bf16[16,16,16,256]{3,2,1,0:T(8,128)(2,1)} custom-call(bf16[3,128,16,128]{3,2,1,0:T(8,128)(2,1)} %bitcast.30, bf16[256,256]{1,0:T(8,128)(2,1)} %bitcast.39, f32[1,256]{1,0:T(1,128)} %reshape_tile.12.bd1, bf16[2,2,256,256]{3,2,1,0:T(8,128)(2,1)} %bitcast.36, f32[1,256]{1,0:T(1,128)} %reshape_tile.13.bc1, bf16[3,2,256,256]{3,2,1,0:T(8,128)(2,1)} %bitcast.32, ...), custom_call_target="tpu_custom_call" | custom-call | tf_op jit(solution)/shard_map/encoder/pallas_call | solution.py:292
  90.2 4.1 %copy.20 = bf16[16,16,16,256]{3,2,1,0:T(8,128)(2,1)} copy(bf16[16,16,16,256]{3,0,1,2:T(8,128)(2,1)} %bitcast.29) | data formatting | bytes 4194304 | tf_op jit(solution)/shard_map/transpose | solution.py:317
  (1 shorter events, 0.0 us)
Async XLA Ops:
  5.0 3.8 %copy-start.3 = (bf16[4,4,64,128]{3,2,1,0:T(8,128)(2,1)S(1)}, bf16[4,4,64,128]{3,2,1,0:T(8,128)(2,1)}, u32[]{:S(2)}) copy-start(bf16[4,4,64,128]{3,2,1,0:T(8,128)(2,1)} %param.18) | copy-start | bytes 786436
  8.9 1.1 %copy-start.2 = (bf16[3,3,128,128]{3,2,1,0:T(8,128)(2,1)S(1)}, bf16[3,3,128,128]{3,2,1,0:T(8,128)(2,1)}, u32[]{:S(2)}) copy-start(bf16[3,3,128,128]{3,2,1,0:T(8,128)(2,1)} %param.20) | copy-start | bytes 884740
  9.9 1.5 %copy-start.1 = (bf16[4,4,128,256]{3,2,1,0:T(8,128)(2,1)S(1)}, bf16[4,4,128,256]{3,2,1,0:T(8,128)(2,1)}, u32[]{:S(2)}) copy-start(bf16[4,4,128,256]{3,2,1,0:T(8,128)(2,1)} %param.22) | copy-start | bytes 3145732
  10.0 2.5 %copy-start = (bf16[16,128,128,3]{2,1,3,0:T(8,128)(2,1)S(1)}, bf16[16,128,128,3]{2,1,3,0:T(8,128)(2,1)}, u32[]{:S(2)}) copy-start(bf16[16,128,128,3]{2,1,3,0:T(8,128)(2,1)} %param.13) | copy-start | bytes 4718596

commit v2 on v0

v2 whole, which is shorter than its diff:
```python
import functools

import jax
import jax.numpy as jnp
from jax import lax
from jax.experimental import pallas as pl
from jax.experimental.pallas import tpu as pltpu
from jax.sharding import PartitionSpec as P

MESH = pl.DeviceIdType.MESH
F32 = jnp.float32
BF16 = jnp.bfloat16

N = 16
L = 128
C = 256
PIX = 640


def body(rows, cols, x_hbm, w_down1, b_down1, w_conv1_hbm, b_conv1, w_down2_hbm, b_down2, w_conv2_hbm, b_conv2, w_down3, b_down3,
         w_conv3, b_conv3, out_hbm, x_ref, w_conv1, w_down2, w_conv2, top, bot, tt, send_l, send_r, recv_l, recv_r, y1, z1, y2, z2, y3,
         wd1, wc1, wd2, wc2, wd3, wc3, biases, turn, out_ref, ssem, rsem, wsem, osem):
    r = lax.axis_index('row')
    c = lax.axis_index('col')
    has_up, has_dn = r > 0, r < rows - 1
    has_lf, has_rt = c > 0, c < cols - 1

    loads = [pltpu.make_async_copy(src, dst, wsem.at[k]) for k, (src, dst) in enumerate((
        (x_hbm, x_ref), (w_conv1_hbm, w_conv1), (w_down2_hbm, w_down2), (w_conv2_hbm, w_conv2), (w_down3, wd3), (w_conv3, wc3)))]
    for copy in loads:
        copy.start()

    neighbours = []
    for dr in (-1, 0, 1):
        for dc in (-1, 0, 1):
            if dr == 0 and dc == 0:
                continue
            there = None
            if dr:
                there = has_up if dr < 0 else has_dn
            if dc:
                side = has_lf if dc < 0 else has_rt
                there = side if there is None else jnp.logical_and(there, side)
            neighbours.append((dr, dc, there))

    def device(dr, dc):
        return {'row': r + dr, 'col': c + dc}

    barrier = pltpu.get_barrier_semaphore()
    for dr, dc, there in neighbours:
        @pl.when(there)
        def _():
            pl.semaphore_signal(barrier, inc=1, device_id=device(dr, dc), device_id_type=MESH)
    n_r = has_up.astype(jnp.int32) + has_dn.astype(jnp.int32)
    n_c = has_lf.astype(jnp.int32) + has_rt.astype(jnp.int32)
    pl.semaphore_wait(barrier, (n_r + 1) * (n_c + 1) - 1)

    def remote(src, dst, k, dr, dc):
        return pltpu.make_async_remote_copy(src_ref=src, dst_ref=dst, send_sem=ssem.at[k], recv_sem=rsem.at[k],
                                            device_id=device(dr, dc), device_id_type=MESH)

    to_dn = remote(x_ref.at[:, L - 8:L], top, 0, 1, 0)
    to_up = remote(x_ref.at[:, 0:8], bot, 1, -1, 0)
    loads[0].wait()

    @pl.when(has_dn)
    def _():
        to_dn.start()

    @pl.when(has_up)
    def _():
        to_up.start()

    def clear(ref, there, index):
        @pl.when(jnp.logical_not(there))
        def _():
            ref[index] = jnp.zeros_like(ref[index])

    every = slice(None)
    clear(top, has_up, (every,))
    clear(bot, has_dn, (every,))
    for copy in loads[1:4]:
        copy.wait()
    pack_weights(w_down1, w_conv1, w_down2, w_conv2, wd1, wc1, wd2, wc2)
    for k, b in enumerate((b_down1, b_conv1, b_down2, b_conv2, b_down3, b_conv3)):
        biases[k:k + 1, :] = jnp.concatenate([b[...]] * (C // b.shape[1]), axis=1)

    def put(cu, g, stack):
        t = jnp.transpose(stack.astype(F32))
        lanes = slice(g * L, g * L + L)
        tt[cu, 5:5 + L, lanes] = t
        send_l[cu, :, lanes] = t[0:8].astype(BF16)
        send_r[cu, :, lanes] = t[L - 8:L].astype(BF16)

    def inner(ch, _):
        for u in range(4):
            for g in (1, 2, 3):
                h0 = 32 * g + u - 5
                put(ch * 4 + u, g, jnp.concatenate([x_ref[ch, h0 + 4 * k] for k in range(8)], axis=0))
        return 0

    lax.fori_loop(0, 3, inner, 0)

    @pl.when(has_up)
    def _():
        to_up.wait_send()
        to_dn.wait_recv()

    @pl.when(has_dn)
    def _():
        to_dn.wait_send()
        to_up.wait_recv()

    def outer(ch, _):
        for u in range(4):
            for g in (0, 4):
                pieces = []
                for k in range(8):
                    h = 32 * g + u - 5 + 4 * k
                    if h < 0:
                        pieces.append(top[ch, h + 8])
                    elif h < L:
                        pieces.append(x_ref[ch, h])
                    elif h < L + 8:
                        pieces.append(bot[ch, h - L])
                    else:
                        pieces.append(jnp.zeros((N, L), BF16))
                put(ch * 4 + u, g, jnp.concatenate(pieces, axis=0))
        return 0

    lax.fori_loop(0, 3, outer, 0)

    to_lf = remote(send_l, recv_r, 2, 0, -1)
    to_rt = remote(send_r, recv_l, 3, 0, 1)

    @pl.when(has_lf)
    def _():
        to_lf.start()

    @pl.when(has_rt)
    def _():
        to_rt.start()

    def dots(pairs):
        acc = None
        for lhs, w in pairs:
            d = jnp.dot(lhs, w, preferred_element_type=F32)
            acc = d if acc is None else acc + d
        return acc

    def finish(acc, k, shape):
        return jnp.maximum(acc + biases[k:k + 1, :], 0.0).astype(BF16).reshape(shape)

    def loop(start, stop, unroll, step):
        assert (stop - start) % unroll == 0

        def run(t, _):
            for e in range(unroll):
                step(start + t * unroll + e)
            return 0

        lax.fori_loop(0, (stop - start) // unroll, run, 0)

    def down1(k):
        win = tt[:, pl.ds(8 * k if isinstance(k, int) else pl.multiple_of(8 * k, 8), N), :]
        for e in range(2):
            xt = jnp.transpose(win[:, 4 * e:4 * e + 8].reshape(96, PIX).astype(BF16))
            xb = jnp.concatenate([xt, jnp.zeros((PIX, L - 96), BF16)], axis=1)
            m = 34 * N
            lhs = jnp.concatenate([xb[0:m], xb[N:N + m]], axis=1)
            y1[2 * k + e] = finish(dots([(lhs, wd1[...])]), 0, (34, N, C))

    def conv1(b):
        pairs = [(y1[b + dw, dh:dh + 33].reshape(33 * N, C), wc1[dw, dh]) for dw in range(2) for dh in range(2)]
        z1[b] = finish(dots(pairs), 1, (33, N, C))

    loop(1, 16, 5, down1)
    clear(y1, has_up, (slice(2, 32), slice(0, 1)))
    clear(y1, has_dn, (slice(2, 32), slice(33, 34)))
    loop(2, 30, 7, conv1)

    @pl.when(has_lf)
    def _():
        to_lf.wait_send()
        to_rt.wait_recv()

    @pl.when(has_rt)
    def _():
        to_rt.wait_send()
        to_lf.wait_recv()

    clear(recv_l, has_lf, (every,))
    clear(recv_r, has_rt, (every,))
    tt[:, 0:5, :] = recv_l[...].astype(F32)[:, 3:8]
    tt[:, 5 + L:13 + L, :] = recv_r[...].astype(F32)
    down1(0)
    down1(N)
    for part in (slice(0, 2), slice(32, 34)):
        clear(y1, has_up, (part, slice(0, 1)))
        clear(y1, has_dn, (part, slice(33, 34)))
    clear(y1, has_lf, (slice(0, 1),))
    clear(y1, has_rt, (slice(33, 34),))
    for b in (0, 1, 30, 31, 32):
        conv1(b)
    clear(z1, has_up, (every, slice(0, 1), every, slice(0, L)))
    clear(z1, has_dn, (every, slice(32, 33), every, slice(L, C)))
    for half in (0, L):
        clear(z1, has_lf, (slice(0, 1), every, every, slice(half, half + 64)))
        clear(z1, has_rt, (slice(32, 33), every, every, slice(half + 64, half + L)))

    def edge(d, around, size, step):
        first, last = around, around + size
        if d == 0:
            return slice(first, last), slice(first, last)
        if d > 0:
            return slice(last - step, last), slice(first - step, first)
        return slice(first, first + step), slice(last, last + step)

    def start(copies):
        for copy, there, _ in copies:
            @pl.when(there)
            def _():
                copy.start()

    def finished(copies):
        for copy, there, back in copies:
            @pl.when(there)
            def _():
                copy.wait_send()
                back.wait_recv()

    def exchange(ref, k0, w_axis, h_axis, wanted):
        made = {}
        for k, (dr, dc, there) in enumerate(neighbours):
            if wanted(dr, dc):
                (ws, wd), (hs, hd) = edge(dc, *w_axis), edge(dr, *h_axis)
                made[k] = (remote(ref.at[ws, hs], ref.at[wd, hd], k0 + k, dr, dc), there)
        return [(copy, there, made[7 - k][0]) for k, (copy, there) in made.items()]

    def sideways(dr, dc):
        return dc != 0

    def upright(dr, dc):
        return dc == 0

    y2_cols = exchange(y2, 4, (1, N, 1), (2, 32, 2), sideways)
    y2_rows = [exchange(y2, k0, (w0, 8, 1), (2, 32, 2), upright) for k0, w0 in ((4, 1), (12, 9))]
    y3_cols = exchange(y3, 20, (1, N, 1), (1, N, 1), sideways)
    y3_rows = exchange(y3, 20, (1, N, 1), (1, N, 1), upright)

    def down2(p):
        pairs = [(z1[2 * p + dw, dh:dh + 32].reshape(32 * N, C), wd2[dw, dh]) for dw in range(3) for dh in range(2)]
        y2[p + 1, 2:34] = finish(dots(pairs), 2, (32, N, C))

    def conv2(q):
        pairs = [(y2[q + dw, dh:dh + 34].reshape(34 * N, C), wc2[dw, dh]) for dw in range(2) for dh in range(3)]
        z2[q] = finish(dots(pairs), 3, (34, N, C))

    for ref, step, last in ((y2, 2, 34), (y3, 1, 17)):
        clear(ref, has_up, (every, slice(0, step)))
        clear(ref, has_dn, (every, slice(last, last + step)))
        clear(ref, has_lf, (slice(0, 1),))
        clear(ref, has_rt, (slice(17, 18),))
    down2(0)
    down2(N - 1)
    start(y2_cols)
    loop(1, 8, 7, down2)
    start(y2_rows[0])
    loop(8, N - 1, 7, down2)
    start(y2_rows[1])
    finished(y2_rows[0])
    loop(1, 8, 7, conv2)
    finished(y2_rows[1])
    loop(8, N, 4, conv2)
    finished(y2_cols)
    conv2(0)
    conv2(N)
    clear(z2, has_up, (every, slice(0, 1)))
    clear(z2, has_dn, (every, slice(33, 34)))
    clear(z2, has_lf, (slice(0, 1), every, every, slice(0, L)))
    clear(z2, has_rt, (slice(N, N + 1), every, every, slice(L, C)))
    for copy in loads[4:]:
        copy.wait()

    def down3(k):
        pairs = []
        for dw in range(2):
            for dh in range(4):
                lhs = [z2[2 * k + e + dw, dh + 2 * i] for e in range(2) for i in range(N)]
                pairs.append((jnp.concatenate(lhs, axis=0), wd3[dh, 2 * dw:2 * dw + 2].reshape(C, C)))
        y3[pl.ds(2 * k + 1, 2), 1:17] = finish(dots(pairs), 4, (2, N, N, C))

    down3(0)
    down3(7)
    start(y3_cols)
    loop(1, 7, 3, down3)
    start(y3_rows)

    def conv3(pair, slot):
        pairs = []
        for dw in range(3):
            for dh in range(3):
                lhs = [y3[dw:dw + N, i + dh].reshape(C, C) for i in pair]
                pairs.append((jnp.concatenate(lhs, axis=0), wc3[dh, dw]))
        res = jnp.maximum(dots(pairs) + biases[5:6, :], 0.0)
        for e, i in enumerate(pair):
            at = 2 * slot + e
            for j in range(N):
                for half in range(2):
                    row = (N * e + j) * N
                    turn[at, half, pl.ds(j, N, stride=17), :] = res[row:row + N, half * L:half * L + L]
            for n in range(N):
                both = [turn[at, half, 17 * n:17 * n + N, :] for half in range(2)]
                out_ref[n, i] = jnp.concatenate(both, axis=1).astype(BF16)

    def put_out(i, size, k):
        return pltpu.make_async_copy(out_ref.at[:, pl.ds(i, size)], out_hbm.at[:, pl.ds(i, size)], osem.at[k])

    finished(y3_cols)

    def conv3_inner(t, _):
        for e in range(3):
            i = 6 * t + 2 * e + 1
            conv3((i, i + 1), e)
        put_out(6 * t + 1, 6, t).start()
        return 0

    lax.fori_loop(0, 2, conv3_inner, 0)
    finished(y3_rows)
    conv3((13, 14), 0)
    conv3((0, 15), 1)
    writes = [put_out(1, 6, 0), put_out(7, 6, 1), put_out(0, 1, 2), put_out(13, 3, 3)]
    for copy in writes[2:]:
        copy.start()
    for copy in writes:
        copy.wait()


def pack_weights(w_down1, w_conv1, w_down2, w_conv2, wd1, wc1, wd2, wc2):
    for dh in range(2):
        blocks = []
        for ch in range(3):
            for u in range(4):
                across = []
                for eh in range(2):
                    for ew in range(2):
                        kh = 4 * dh + u - 2 * eh
                        if 0 <= kh < 4:
                            down = [w_down1[kh, ch].astype(F32), jnp.zeros((4 - 2 * ew, 64), F32)]
                            across.append(jnp.concatenate(([jnp.zeros((2, 64), F32)] if ew else []) + down, axis=0))
                        else:
                            across.append(jnp.zeros((8, 64), F32))
                blocks.append(jnp.concatenate(across, axis=1))
        blocks.append(jnp.zeros((32, C), F32))
        wd1[L * dh:L * dh + L, :] = jnp.concatenate(blocks, axis=0).astype(BF16)
    for dw in range(2):
        for mw in range(2):
            for dh in range(2):
                for mh in range(2):
                    across = []
                    for eh in range(2):
                        for ew in range(2):
                            kh, kw = 2 * dh + mh - eh, 2 * dw + mw - ew
                            inside = 0 <= kh < 3 and 0 <= kw < 3
                            across.append(w_conv1[kh, kw] if inside else jnp.zeros((64, 64), BF16))
                    at = (2 * mh + mw) * 64
                    wc1[dw, dh, at:at + 64, :] = jnp.concatenate(across, axis=1)
    for dw in range(3):
        for mw in range(2):
            for dh in range(2):
                for mh in range(2):
                    at = (2 * mh + mw) * 64
                    for ew in range(2):
                        kw = 2 * dw + mw - 2 * ew
                        value = w_down2[2 * dh + mh, kw] if 0 <= kw < 4 else jnp.zeros((64, L), BF16)
                        wd2[dw, dh, at:at + 64, L * ew:L * ew + L] = value
    for dw in range(2):
        for mw in range(2):
            for kh in range(3):
                for ew in range(2):
                    kw = 2 * dw + mw - ew
                    value = w_conv2[kh, kw] if 0 <= kw < 3 else jnp.zeros((L, L), BF16)
                    wc2[dw, kh, L * mw:L * mw + L, L * ew:L * ew + L] = value


def solution(mesh):
    rows, cols = mesh.shape['row'], mesh.shape['col']

    def local(images, w_down1, b_down1, w_conv1, b_conv1, w_down2, b_down2, w_conv2, b_conv2, w_down3, b_down3, w_conv3, b_conv3):
        x = jnp.transpose(images, (3, 1, 0, 2))

        def row(b):
            return b.reshape(1, -1)

        def act(w, h):
            return pltpu.VMEM((w, h, N, C), BF16)

        vmem = pl.BlockSpec(memory_space=pltpu.VMEM)
        hbm = pl.BlockSpec(memory_space=pl.ANY)
        strip = pltpu.VMEM((12, 8, PIX), BF16)
        weight_in = [pltpu.VMEM(w.shape, BF16) for w in (w_conv1, w_down2, w_conv2)]
        weights = [pltpu.VMEM(shape, BF16) for shape in
                   ((C, C), (2, 2, C, C), (3, 2, C, C), (2, 3, C, C), w_down3.shape, w_conv3.shape)]
        dma = pltpu.SemaphoreType.DMA
        return pl.pallas_call(
            functools.partial(body, rows, cols),
            out_shape=jax.ShapeDtypeStruct((N, N, N, C), BF16),
            in_specs=[hbm, vmem, vmem] + [hbm, vmem] * 5,
            out_specs=hbm,
            scratch_shapes=[pltpu.VMEM((3, L, N, L), BF16)] + weight_in + [pltpu.VMEM((3, 8, N, L), BF16)] * 2
            + [pltpu.VMEM((12, 144, PIX), F32)] + [strip] * 4
            + [act(34, 34), act(33, 33), act(18, 36), act(17, 34), act(18, 18)] + weights
            + [pltpu.VMEM((8, C), F32), pltpu.VMEM((6, 2, 17 * N, L), F32), act(N, N), dma((28,)), dma((28,)), dma((6,)), dma((4,))],
            compiler_params=pltpu.CompilerParams(collective_id=0, has_side_effects=True, vmem_limit_bytes=66_000_000),
            name='encoder',
        )(x, jnp.transpose(w_down1, (0, 2, 1, 3)), row(b_down1), w_conv1, row(b_conv1), w_down2, row(b_down2), w_conv2, row(b_conv2),
          w_down3, row(b_down3), w_conv3, row(b_conv3))

    tile_spec = P('batch', 'row', 'col', None)
    return jax.shard_map(local, mesh=mesh, in_specs=(tile_spec,) + (P(),) * 12, out_specs=tile_spec, check_vma=False)
```

time: 277 us -> 57.7 us (0.21)
  matrix products: 142 us -> 0 us
  starting transfers between devices: 55.7 us -> 0 us
  waiting for transfers between devices: 53.1 us -> 0 us
  Pallas kernels: 0 us -> 50.8 us
  local copies, waits for them, and re-layouts: 21.5 us -> 6.66 us
    conv_general_dilated x6 -> x0, matrix products: 142 us -> none  [conv_relu(): lax.conv_general_dilated(padded, weight, (stride, stride), 'VALID', dimen...]
    ppermute x24 -> x0, starting transfers between devices: 55.7 us -> none  [the longest x12 35.2 us: add_halo(): from_prev = lax.ppermute(tail_edge, axis_name, to_next)]
    ppermute x24 -> x0, waiting for transfers between devices: 53.1 us -> none  [the longest x12 45.4 us: add_halo(): from_next = lax.ppermute(head_edge, axis_name, to_prev)]
    pallas_call x0 -> x1, Pallas kernels: none -> 50.8 us  [local(): pl.pallas_call(functools.partial(body, rows, cols), out_shape=jax.ShapeDt...]
    unnamed x27 -> x2, local copies, waits for them, and re-layouts: 16.4 us -> 6.66 us
    slice x10 -> x0, local copies, waits for them, and re-layouts: 2.78 us -> none  [the longest x7 2.38 us: add_halo(): tail_edge = act_tile[:, -1:]]
  transfers between devices with their start and end apart: 24 -> 0, of which waited for: 18 -> 0; matrix products, arithmetic and copies ran while one was open for 6% -> 0% of each run, Pallas kernels for 0% -> 0%
where the time goes in v2:
time: 57.7 us; the launch traced here: 57.5 us
  Pallas kernels  50.8 us (88%)
  local copies, waits for them, and re-layouts  6.66 us (12%)
    pallas_call x1, Pallas kernels, local(): pl.pallas_call(functools.partial(body, rows, cols), out_shape=jax.ShapeDt...  50.8 us
    unnamed x2, local copies, waits for them, and re-layouts  6.66 us

profile of v2, /device:TPU:1, one launch (start us, length us, event | category | flops | bytes accessed | tf_op | source)
XLA Modules:
  0.0 57.5 jit_solution(6909142050596976972)
XLA Ops:
  0.0 3.6 %copy.16 = bf16[16,128,128,3]{2,0,1,3:T(8,128)(2,1)} copy(bf16[16,128,128,3]{2,1,3,0:T(8,128)(2,1)} %param.13) | data formatting | bytes 3145728 | tf_op args[0]
  3.6 50.8 %encoder.1 = bf16[16,16,16,256]{3,2,1,0:T(8,128)(2,1)} custom-call(bf16[3,128,16,128]{3,2,1,0:T(8,128)(2,1)} %bitcast.10, bf16[4,3,4,64]{3,2,1,0:T(4,128)(2,1)} %bitcast.11, f32[1,64]{1,0:T(1,128)} %bitcast.14, bf16[3,3,64,64]{3,2,1,0:T(8,128)(2,1)} %w_conv1_hbm.1, f32[1,64]{1,0:T(1,128)} %bitcast.15, bf16[4,4,64,128]{3,2,1,0:T(8,128)(2,1)} %w_down2_hbm.1, ...), custom_call_target="tpu_custom_call" | custom-call | tf_op jit(solution)/shard_map/encoder/pallas_call | solution.py:405
  54.4 3.1 %copy.18 = bf16[16,16,16,256]{3,2,1,0:T(8,128)(2,1)} copy(bf16[16,16,16,256]{3,2,1,0:T(8,128)(2,1)} %encoder.1) | data formatting | bytes 4194304

commit v3 on v2

--- a/solution.py
+++ b/solution.py
@@ -18,7 +18,7 @@
 
 
 def body(rows, cols, x_hbm, w_down1, b_down1, w_conv1_hbm, b_conv1, w_down2_hbm, b_down2, w_conv2_hbm, b_conv2, w_down3, b_down3,
-         w_conv3, b_conv3, out_hbm, x_ref, w_conv1, w_down2, w_conv2, top, bot, tt, send_l, send_r, recv_l, recv_r, y1, z1, y2, z2, y3,
+         w_conv3, b_conv3, out_hbm, x_ref, w_conv1, w_down2, w_conv2, top, bot, xs, tt, send_l, send_r, recv_l, recv_r, y1, z1, y2, z2, y3,
          wd1, wc1, wd2, wc2, wd3, wc3, biases, turn, out_ref, ssem, rsem, wsem, osem):
     r = lax.axis_index('row')
     c = lax.axis_index('col')
@@ -59,8 +59,8 @@
         return pltpu.make_async_remote_copy(src_ref=src, dst_ref=dst, send_sem=ssem.at[k], recv_sem=rsem.at[k],
                                             device_id=device(dr, dc), device_id_type=MESH)
 
-    to_dn = remote(x_ref.at[:, L - 8:L], top, 0, 1, 0)
-    to_up = remote(x_ref.at[:, 0:8], bot, 1, -1, 0)
+    to_dn = remote(x_ref.at[:, :, L - 8:L], top, 0, 1, 0)
+    to_up = remote(x_ref.at[:, :, 0:8], bot, 1, -1, 0)
     loads[0].wait()
 
     @pl.when(has_dn)
@@ -85,18 +85,27 @@
     for k, b in enumerate((b_down1, b_conv1, b_down2, b_conv2, b_down3, b_conv3)):
         biases[k:k + 1, :] = jnp.concatenate([b[...]] * (C // b.shape[1]), axis=1)
 
-    def put(cu, g, stack):
-        t = jnp.transpose(stack.astype(F32))
-        lanes = slice(g * L, g * L + L)
-        tt[cu, 5:5 + L, lanes] = t
-        send_l[cu, :, lanes] = t[0:8].astype(BF16)
-        send_r[cu, :, lanes] = t[L - 8:L].astype(BF16)
+    def gather(ch, src, h, size):
+        for n in range(N):
+            xs[ch, pl.ds(17 * (h + 8) + n, size, stride=17), :] = src[n, ch].astype(F32)
+
+    def put(ch, g):
+        for u in range(4):
+            pieces = []
+            for k in range(8):
+                at = 17 * (32 * g + u + 3 + 4 * k)
+                pieces.append(xs[ch, at:at + N, :] if at < 17 * (L + N) else jnp.zeros((N, L), F32))
+            t = jnp.transpose(jnp.concatenate(pieces, axis=0))
+            cu = ch * 4 + u
+            lanes = slice(g * L, g * L + L)
+            tt[cu, 5:5 + L, lanes] = t
+            send_l[cu, :, lanes] = t[0:8].astype(BF16)
+            send_r[cu, :, lanes] = t[L - 8:L].astype(BF16)
 
     def inner(ch, _):
-        for u in range(4):
-            for g in (1, 2, 3):
-                h0 = 32 * g + u - 5
-                put(ch * 4 + u, g, jnp.concatenate([x_ref[ch, h0 + 4 * k] for k in range(8)], axis=0))
+        gather(ch, x_ref, 0, L)
+        for g in (1, 2, 3):
+            put(ch, g)
         return 0
 
     lax.fori_loop(0, 3, inner, 0)
@@ -112,20 +121,10 @@
         to_up.wait_recv()
 
     def outer(ch, _):
-        for u in range(4):
-            for g in (0, 4):
-                pieces = []
-                for k in range(8):
-                    h = 32 * g + u - 5 + 4 * k
-                    if h < 0:
-                        pieces.append(top[ch, h + 8])
-                    elif h < L:
-                        pieces.append(x_ref[ch, h])
-                    elif h < L + 8:
-                        pieces.append(bot[ch, h - L])
-                    else:
-                        pieces.append(jnp.zeros((N, L), BF16))
-                put(ch * 4 + u, g, jnp.concatenate(pieces, axis=0))
+        gather(ch, top, -8, 8)
+        gather(ch, bot, L, 8)
+        for g in (0, 4):
+            put(ch, g)
         return 0
 
     lax.fori_loop(0, 3, outer, 0)
@@ -177,7 +176,7 @@
     loop(1, 16, 5, down1)
     clear(y1, has_up, (slice(2, 32), slice(0, 1)))
     clear(y1, has_dn, (slice(2, 32), slice(33, 34)))
-    loop(2, 30, 7, conv1)
+    loop(2, 30, 14, conv1)
 
     @pl.when(has_lf)
     def _():
@@ -271,7 +270,7 @@
     finished(y2_rows[0])
     loop(1, 8, 7, conv2)
     finished(y2_rows[1])
-    loop(8, N, 4, conv2)
+    loop(8, N, 8, conv2)
     finished(y2_cols)
     conv2(0)
     conv2(N)
@@ -293,7 +292,7 @@
     down3(0)
     down3(7)
     start(y3_cols)
-    loop(1, 7, 3, down3)
+    loop(1, 7, 6, down3)
     start(y3_rows)
 
     def conv3(pair, slot):
@@ -302,7 +301,7 @@
             for dh in range(3):
                 lhs = [y3[dw:dw + N, i + dh].reshape(C, C) for i in pair]
                 pairs.append((jnp.concatenate(lhs, axis=0), wc3[dh, dw]))
-        res = jnp.maximum(dots(pairs) + biases[5:6, :], 0.0)
+        res = dots(pairs) + biases[5:6, :]
         for e, i in enumerate(pair):
             at = 2 * slot + e
             for j in range(N):
@@ -387,7 +386,7 @@
     rows, cols = mesh.shape['row'], mesh.shape['col']
 
     def local(images, w_down1, b_down1, w_conv1, b_conv1, w_down2, b_down2, w_conv2, b_conv2, w_down3, b_down3, w_conv3, b_conv3):
-        x = jnp.transpose(images, (3, 1, 0, 2))
+        x = jnp.transpose(images, (0, 3, 1, 2))
 
         def row(b):
             return b.reshape(1, -1)
@@ -402,19 +401,20 @@
         weights = [pltpu.VMEM(shape, BF16) for shape in
                    ((C, C), (2, 2, C, C), (3, 2, C, C), (2, 3, C, C), w_down3.shape, w_conv3.shape)]
         dma = pltpu.SemaphoreType.DMA
-        return pl.pallas_call(
+        out = pl.pallas_call(
             functools.partial(body, rows, cols),
             out_shape=jax.ShapeDtypeStruct((N, N, N, C), BF16),
             in_specs=[hbm, vmem, vmem] + [hbm, vmem] * 5,
             out_specs=hbm,
-            scratch_shapes=[pltpu.VMEM((3, L, N, L), BF16)] + weight_in + [pltpu.VMEM((3, 8, N, L), BF16)] * 2
-            + [pltpu.VMEM((12, 144, PIX), F32)] + [strip] * 4
+            scratch_shapes=[pltpu.VMEM((N, 3, L, L), BF16)] + weight_in + [pltpu.VMEM((N, 3, 8, L), BF16)] * 2
+            + [pltpu.VMEM((3, 17 * (L + N), L), F32), pltpu.VMEM((12, 144, PIX), F32)] + [strip] * 4
             + [act(34, 34), act(33, 33), act(18, 36), act(17, 34), act(18, 18)] + weights
             + [pltpu.VMEM((8, C), F32), pltpu.VMEM((6, 2, 17 * N, L), F32), act(N, N), dma((28,)), dma((28,)), dma((6,)), dma((4,))],
             compiler_params=pltpu.CompilerParams(collective_id=0, has_side_effects=True, vmem_limit_bytes=66_000_000),
             name='encoder',
         )(x, jnp.transpose(w_down1, (0, 2, 1, 3)), row(b_down1), w_conv1, row(b_conv1), w_down2, row(b_down2), w_conv2, row(b_conv2),
           w_down3, row(b_down3), w_conv3, row(b_conv3))
+        return jnp.maximum(out, jnp.zeros_like(out))
 
     tile_spec = P('batch', 'row', 'col', None)
     return jax.shard_map(local, mesh=mesh, in_specs=(tile_spec,) + (P(),) * 12, out_specs=tile_spec, check_vma=False)

time: 57.7 us -> 53.7 us (0.931)
  local copies, waits for them, and re-layouts: 6.66 us -> 0 us
  other arithmetic: 0 us -> 3.05 us
    unnamed x2 -> x0, local copies, waits for them, and re-layouts: 6.66 us -> none
    max x0 -> x1, other arithmetic: none -> 3.05 us  [local(): return jnp.maximum(out, jnp.zeros_like(out))]
where the time goes in v3:
time: 53.7 us; the launch traced here: 53.5 us
  Pallas kernels  50.5 us (94%)
  other arithmetic  3.05 us (6%)
    pallas_call x1, Pallas kernels, local(): pl.pallas_call(functools.partial(body, rows, cols), out_shape=jax.ShapeDt...  50.5 us
    max x1, other arithmetic, local(): return jnp.maximum(out, jnp.zeros_like(out))  3.05 us

profile of v3, /device:TPU:1, one launch (start us, length us, event | category | flops | bytes accessed | tf_op | source)
XLA Modules:
  0.0 53.5 jit_solution(356005958902948756)
XLA Ops:
  0.0 50.5 %encoder.1 = bf16[16,16,16,256]{3,2,1,0:T(8,128)(2,1)} custom-call(bf16[16,3,128,128]{3,2,1,0:T(8,128)(2,1)} %bitcast.8, bf16[4,3,4,64]{3,2,1,0:T(4,128)(2,1)} %bitcast.9, f32[1,64]{1,0:T(1,128)} %bitcast.12, bf16[3,3,64,64]{3,2,1,0:T(8,128)(2,1)} %w_conv1_hbm.1, f32[1,64]{1,0:T(1,128)} %bitcast.13, bf16[4,4,64,128]{3,2,1,0:T(8,128)(2,1)} %w_down2_hbm.1, ...), custom_call_target="tpu_custom_call" | custom-call | tf_op jit(solution)/shard_map/encoder/pallas_call | solution.py:404
  50.5 3.0 %broadcast_maximum_fusion = bf16[16,16,16,256]{3,2,1,0:T(8,128)(2,1)} fusion(bf16[16,16,16,256]{3,2,1,0:T(8,128)(2,1)} %encoder.1), kind=kLoop, calls=%fused_computation | loop fusion | flops 1048576 | bytes 4194304 | tf_op jit(solution)/shard_map/max | solution.py:417

commit v4 on v3

--- a/solution.py
+++ b/solution.py
@@ -48,12 +48,13 @@
 
     barrier = pltpu.get_barrier_semaphore()
     for dr, dc, there in neighbours:
+        if dr and dc:
+            continue
+
         @pl.when(there)
         def _():
             pl.semaphore_signal(barrier, inc=1, device_id=device(dr, dc), device_id_type=MESH)
-    n_r = has_up.astype(jnp.int32) + has_dn.astype(jnp.int32)
-    n_c = has_lf.astype(jnp.int32) + has_rt.astype(jnp.int32)
-    pl.semaphore_wait(barrier, (n_r + 1) * (n_c + 1) - 1)
+    pl.semaphore_wait(barrier, sum(t.astype(jnp.int32) for t in (has_up, has_dn, has_lf, has_rt)))
 
     def remote(src, dst, k, dr, dc):
         return pltpu.make_async_remote_copy(src_ref=src, dst_ref=dst, send_sem=ssem.at[k], recv_sem=rsem.at[k],
@@ -255,6 +256,20 @@
         pairs = [(y2[q + dw, dh:dh + 34].reshape(34 * N, C), wc2[dw, dh]) for dw in range(2) for dh in range(3)]
         z2[q] = finish(dots(pairs), 3, (34, N, C))
 
+    def conv2_inner(q):
+        pairs = [(y2[q + dw, dh + 2:dh + 32].reshape(30 * N, C), wc2[dw, dh]) for dw in range(2) for dh in range(3)]
+        z2[q, 2:32] = finish(dots(pairs), 3, (30, N, C))
+
+    def conv2_rest(first, last):
+        pairs = []
+        for dw in range(2):
+            for dh in range(3):
+                lhs = [y2[q + dw, h + dh:h + dh + 2].reshape(2 * N, C) for q in range(first, last) for h in (0, 32)]
+                pairs.append((jnp.concatenate(lhs, axis=0), wc2[dw, dh]))
+        res = finish(dots(pairs), 3, (last - first, 4, N, C))
+        z2[first:last, 0:2] = res[:, 0:2]
+        z2[first:last, 32:34] = res[:, 2:4]
+
     for ref, step, last in ((y2, 2, 34), (y3, 1, 17)):
         clear(ref, has_up, (every, slice(0, step)))
         clear(ref, has_dn, (every, slice(last, last + step)))
@@ -267,15 +282,17 @@
     start(y2_rows[0])
     loop(8, N - 1, 7, down2)
     start(y2_rows[1])
-    finished(y2_rows[0])
-    loop(1, 8, 7, conv2)
-    finished(y2_rows[1])
-    loop(8, N, 8, conv2)
-    finished(y2_cols)
-    conv2(0)
-    conv2(N)
-    clear(z2, has_up, (every, slice(0, 1)))
-    clear(z2, has_dn, (every, slice(33, 34)))
+    for q in range(3, 12):
+        conv2_inner(q)
+    for copies in (*y2_rows, y2_cols):
+        finished(copies)
+    outer_q = (slice(0, 3), slice(14, 17))
+    for part in outer_q:
+        for q in range(part.start, part.stop):
+            conv2(q)
+    for part in outer_q:
+        clear(z2, has_up, (part, slice(0, 1)))
+        clear(z2, has_dn, (part, slice(33, 34)))
     clear(z2, has_lf, (slice(0, 1), every, every, slice(0, L)))
     clear(z2, has_rt, (slice(N, N + 1), every, every, slice(L, C)))
     for copy in loads[4:]:
@@ -292,7 +309,13 @@
     down3(0)
     down3(7)
     start(y3_cols)
-    loop(1, 7, 6, down3)
+    conv2_inner(12)
+    conv2_inner(13)
+    conv2_rest(3, 14)
+    clear(z2, has_up, (slice(3, 14), slice(0, 1)))
+    clear(z2, has_dn, (slice(3, 14), slice(33, 34)))
+    for k in range(1, 7):
+        down3(k)
     start(y3_rows)
 
     def conv3(pair, slot):
@@ -301,7 +324,7 @@
             for dh in range(3):
                 lhs = [y3[dw:dw + N, i + dh].reshape(C, C) for i in pair]
                 pairs.append((jnp.concatenate(lhs, axis=0), wc3[dh, dw]))
-        res = dots(pairs) + biases[5:6, :]
+        res = jnp.maximum(dots(pairs) + biases[5:6, :], 0.0)
         for e, i in enumerate(pair):
             at = 2 * slot + e
             for j in range(N):
@@ -331,6 +354,19 @@
     writes = [put_out(1, 6, 0), put_out(7, 6, 1), put_out(0, 1, 2), put_out(13, 3, 3)]
     for copy in writes[2:]:
         copy.start()
+    for copy in writes:
+        copy.wait()
+
+
+def hand_on(src, dst, held, isem, osem):
+    parts = [pl.ds(2 * k, 2) for k in range(8)]
+    reads = [pltpu.make_async_copy(src.at[p], held.at[p], isem.at[k]) for k, p in enumerate(parts)]
+    writes = [pltpu.make_async_copy(held.at[p], dst.at[p], osem.at[k]) for k, p in enumerate(parts)]
+    for copy in reads:
+        copy.start()
+    for read, write in zip(reads, writes):
+        read.wait()
+        write.start()
     for copy in writes:
         copy.wait()
 
@@ -414,7 +450,14 @@
             name='encoder',
         )(x, jnp.transpose(w_down1, (0, 2, 1, 3)), row(b_down1), w_conv1, row(b_conv1), w_down2, row(b_down2), w_conv2, row(b_conv2),
           w_down3, row(b_down3), w_conv3, row(b_conv3))
-        return jnp.maximum(out, jnp.zeros_like(out))
+        return pl.pallas_call(
+            hand_on,
+            out_shape=jax.ShapeDtypeStruct(out.shape, BF16),
+            in_specs=[hbm],
+            out_specs=hbm,
+            scratch_shapes=[act(N, N), dma((8,)), dma((8,))],
+            name='hand_on',
+        )(out)
 
     tile_spec = P('batch', 'row', 'col', None)
     return jax.shard_map(local, mesh=mesh, in_specs=(tile_spec,) + (P(),) * 12, out_specs=tile_spec, check_vma=False)

time: 53.7 us -> 52.8 us (0.983)
  other arithmetic: 3.05 us -> 0 us
  Pallas kernels: 50.5 us -> 52.4 us
    max x1 -> x0, other arithmetic: 3.05 us -> none  [local(): return jnp.maximum(out, jnp.zeros_like(out))]
    pallas_call x0 -> x1, Pallas kernels: none -> 2.39 us  [local(): pl.pallas_call(hand_on, out_shape=jax.ShapeDtypeStruct(out.shape, BF16),...]
where the time goes in v4:
time: 52.8 us; the launch traced here: 52.6 us
  Pallas kernels  52.4 us (99%)
    pallas_call x1, Pallas kernels, local(): pl.pallas_call(functools.partial(body, rows, cols), out_shape=jax.ShapeDt...  50 us
    pallas_call x1, Pallas kernels, local(): pl.pallas_call(hand_on, out_shape=jax.ShapeDtypeStruct(out.shape, BF16),...  2.39 us

profile of v4, /device:TPU:1, one launch (start us, length us, event | category | flops | bytes accessed | tf_op | source)
XLA Modules:
  0.0 52.6 jit_solution(8636012025743729692)
XLA Ops:
  0.0 50.0 %encoder.1.src = bf16[16,16,16,256]{3,2,1,0:T(8,128)(2,1)} custom-call(bf16[16,3,128,128]{3,2,1,0:T(8,128)(2,1)} %bitcast.8, bf16[4,3,4,64]{3,2,1,0:T(4,128)(2,1)} %bitcast.9, f32[1,64]{1,0:T(1,128)} %bitcast.12, bf16[3,3,64,64]{3,2,1,0:T(8,128)(2,1)} %w_conv1_hbm.1, f32[1,64]{1,0:T(1,128)} %bitcast.13, bf16[4,4,64,128]{3,2,1,0:T(8,128)(2,1)} %w_down2_hbm.1, ...), custom_call_target="tpu_custom_call" | custom-call | tf_op jit(solution)/shard_map/encoder/pallas_call | solution.py:440
  50.0 2.4 %hand_on.1 = bf16[16,16,16,256]{3,2,1,0:T(8,128)(2,1)} custom-call(bf16[16,16,16,256]{3,2,1,0:T(8,128)(2,1)} %encoder.1.src), custom_call_target="tpu_custom_call" | custom-call | tf_op jit(solution)/shard_map/hand_on/pallas_call | solution.py:453

commit v5 on v4

--- a/solution.py
+++ b/solution.py
@@ -15,10 +15,12 @@
 L = 128
 C = 256
 PIX = 640
+HALF = 64
+PITCH = 17
 
 
 def body(rows, cols, x_hbm, w_down1, b_down1, w_conv1_hbm, b_conv1, w_down2_hbm, b_down2, w_conv2_hbm, b_conv2, w_down3, b_down3,
-         w_conv3, b_conv3, out_hbm, x_ref, w_conv1, w_down2, w_conv2, top, bot, xs, tt, send_l, send_r, recv_l, recv_r, y1, z1, y2, z2, y3,
+         w_conv3, b_conv3, out_hbm, x_ref, w_conv1, w_down2, w_conv2, top, bot, xs, tt, kept, send_l, send_r, recv_l, recv_r, y1, z1, y2, z2, y3,
          wd1, wc1, wd2, wc2, wd3, wc3, biases, turn, out_ref, ssem, rsem, wsem, osem):
     r = lax.axis_index('row')
     c = lax.axis_index('col')
@@ -80,22 +82,20 @@
     every = slice(None)
     clear(top, has_up, (every,))
     clear(bot, has_dn, (every,))
-    for copy in loads[1:4]:
-        copy.wait()
-    pack_weights(w_down1, w_conv1, w_down2, w_conv2, wd1, wc1, wd2, wc2)
+    pack_down1(w_down1, wd1)
     for k, b in enumerate((b_down1, b_conv1, b_down2, b_conv2, b_down3, b_conv3)):
         biases[k:k + 1, :] = jnp.concatenate([b[...]] * (C // b.shape[1]), axis=1)
 
     def gather(ch, src, h, size):
         for n in range(N):
-            xs[ch, pl.ds(17 * (h + 8) + n, size, stride=17), :] = src[n, ch].astype(F32)
+            xs[ch, pl.ds(PITCH * (h + 8) + n, size, stride=PITCH), :] = src[n, ch].astype(F32)
 
     def put(ch, g):
         for u in range(4):
             pieces = []
             for k in range(8):
-                at = 17 * (32 * g + u + 3 + 4 * k)
-                pieces.append(xs[ch, at:at + N, :] if at < 17 * (L + N) else jnp.zeros((N, L), F32))
+                at = PITCH * (32 * g + u + 3 + 4 * k)
+                pieces.append(xs[ch, at:at + N, :] if at < PITCH * (L + N) else jnp.zeros((N, L), F32))
             t = jnp.transpose(jnp.concatenate(pieces, axis=0))
             cu = ch * 4 + u
             lanes = slice(g * L, g * L + L)
@@ -111,6 +111,52 @@
 
     lax.fori_loop(0, 3, inner, 0)
 
+    def dots(pairs):
+        acc = None
+        for lhs, w in pairs:
+            d = jnp.dot(lhs, w, preferred_element_type=F32)
+            acc = d if acc is None else acc + d
+        return acc
+
+    def finish(acc, k, shape):
+        return jnp.maximum(acc + biases[k:k + 1, :], 0.0).astype(BF16).reshape(shape)
+
+    def window(k, e, lanes):
+        size = sum(last - first for first, last in lanes)
+        win = [tt[:, 8 * k:8 * k + N, first:last][:, 4 * e:4 * e + 8].reshape(96, last - first) for first, last in lanes]
+        xt = jnp.transpose(jnp.concatenate(win, axis=1).astype(BF16))
+        return jnp.concatenate([xt, jnp.zeros((size, L - 96), BF16)], axis=1)
+
+    def down1(k):
+        m = 34 * N
+        for e in range(2):
+            xb = window(k, e, [(0, PIX)])
+            lhs = jnp.concatenate([xb[0:m], xb[N:N + m]], axis=1)
+            y1[2 * k + e] = finish(dots([(lhs, wd1[...])]), 0, (34, N, C))
+
+    def down1_inner(k):
+        m = 23 * N
+        for e in range(2):
+            xb = window(k, e, [(L, 4 * L)])
+            kept[2 * k + e, 0] = xb[0:N]
+            kept[2 * k + e, 1] = xb[m:m + N]
+            lhs = jnp.concatenate([xb[0:m], xb[N:N + m]], axis=1)
+            y1[2 * k + e, 8:31] = finish(dots([(lhs, wd1[...])]), 0, (23, N, C))
+
+    def down1_outer(k):
+        lhs = []
+        for e in range(2):
+            xb = window(k, e, [(0, L), (4 * L, PIX)])
+            this = jnp.concatenate([xb[0:L], kept[2 * k + e, 1], xb[L:L + 2 * N]], axis=0)
+            below = jnp.concatenate([xb[N:L], kept[2 * k + e, 0], xb[L:L + 3 * N]], axis=0)
+            lhs.append(jnp.concatenate([this, below], axis=1))
+        res = finish(dots([(jnp.concatenate(lhs, axis=0), wd1[...])]), 0, (2, 11, N, C))
+        y1[2 * k:2 * k + 2, 0:8] = res[:, 0:8]
+        y1[2 * k:2 * k + 2, 31:34] = res[:, 8:11]
+
+    for k in range(1, N):
+        down1_inner(k)
+
     @pl.when(has_up)
     def _():
         to_up.wait_send()
@@ -141,16 +187,6 @@
     def _():
         to_rt.start()
 
-    def dots(pairs):
-        acc = None
-        for lhs, w in pairs:
-            d = jnp.dot(lhs, w, preferred_element_type=F32)
-            acc = d if acc is None else acc + d
-        return acc
-
-    def finish(acc, k, shape):
-        return jnp.maximum(acc + biases[k:k + 1, :], 0.0).astype(BF16).reshape(shape)
-
     def loop(start, stop, unroll, step):
         assert (stop - start) % unroll == 0
 
@@ -161,20 +197,15 @@
 
         lax.fori_loop(0, (stop - start) // unroll, run, 0)
 
-    def down1(k):
-        win = tt[:, pl.ds(8 * k if isinstance(k, int) else pl.multiple_of(8 * k, 8), N), :]
-        for e in range(2):
-            xt = jnp.transpose(win[:, 4 * e:4 * e + 8].reshape(96, PIX).astype(BF16))
-            xb = jnp.concatenate([xt, jnp.zeros((PIX, L - 96), BF16)], axis=1)
-            m = 34 * N
-            lhs = jnp.concatenate([xb[0:m], xb[N:N + m]], axis=1)
-            y1[2 * k + e] = finish(dots([(lhs, wd1[...])]), 0, (34, N, C))
-
     def conv1(b):
         pairs = [(y1[b + dw, dh:dh + 33].reshape(33 * N, C), wc1[dw, dh]) for dw in range(2) for dh in range(2)]
         z1[b] = finish(dots(pairs), 1, (33, N, C))
 
-    loop(1, 16, 5, down1)
+    for copy in loads[1:4]:
+        copy.wait()
+    pack_conv1(w_conv1, wc1)
+    for k in range(1, N):
+        down1_outer(k)
     clear(y1, has_up, (slice(2, 32), slice(0, 1)))
     clear(y1, has_dn, (slice(2, 32), slice(33, 34)))
     loop(2, 30, 14, conv1)
@@ -200,13 +231,14 @@
         clear(y1, has_dn, (part, slice(33, 34)))
     clear(y1, has_lf, (slice(0, 1),))
     clear(y1, has_rt, (slice(33, 34),))
+    pack_stage2(w_down2, w_conv2, wd2, wc2)
     for b in (0, 1, 30, 31, 32):
         conv1(b)
     clear(z1, has_up, (every, slice(0, 1), every, slice(0, L)))
     clear(z1, has_dn, (every, slice(32, 33), every, slice(L, C)))
     for half in (0, L):
-        clear(z1, has_lf, (slice(0, 1), every, every, slice(half, half + 64)))
-        clear(z1, has_rt, (slice(32, 33), every, every, slice(half + 64, half + L)))
+        clear(z1, has_lf, (slice(0, 1), every, every, slice(half, half + HALF)))
+        clear(z1, has_rt, (slice(32, 33), every, every, slice(half + HALF, half + L)))
 
     def edge(d, around, size, step):
         first, last = around, around + size
@@ -330,9 +362,9 @@
             for j in range(N):
                 for half in range(2):
                     row = (N * e + j) * N
-                    turn[at, half, pl.ds(j, N, stride=17), :] = res[row:row + N, half * L:half * L + L]
+                    turn[at, half, pl.ds(j, N, stride=PITCH), :] = res[row:row + N, half * L:half * L + L]
             for n in range(N):
-                both = [turn[at, half, 17 * n:17 * n + N, :] for half in range(2)]
+                both = [turn[at, half, PITCH * n:PITCH * n + N, :] for half in range(2)]
                 out_ref[n, i] = jnp.concatenate(both, axis=1).astype(BF16)
 
     def put_out(i, size, k):
@@ -349,12 +381,13 @@
 
     lax.fori_loop(0, 2, conv3_inner, 0)
     finished(y3_rows)
+    last = [put_out(13, 2, 2), put_out(0, 1, 3), put_out(15, 1, 4)]
     conv3((13, 14), 0)
+    last[0].start()
     conv3((0, 15), 1)
-    writes = [put_out(1, 6, 0), put_out(7, 6, 1), put_out(0, 1, 2), put_out(13, 3, 3)]
-    for copy in writes[2:]:
+    for copy in last[1:]:
         copy.start()
-    for copy in writes:
+    for copy in (put_out(1, 6, 0), put_out(7, 6, 1), *last):
         copy.wait()
 
 
@@ -371,7 +404,7 @@
         copy.wait()
 
 
-def pack_weights(w_down1, w_conv1, w_down2, w_conv2, wd1, wc1, wd2, wc2):
+def pack_down1(w_down1, wd1):
     for dh in range(2):
         blocks = []
         for ch in range(3):
@@ -381,13 +414,16 @@
                     for ew in range(2):
                         kh = 4 * dh + u - 2 * eh
                         if 0 <= kh < 4:
-                            down = [w_down1[kh, ch].astype(F32), jnp.zeros((4 - 2 * ew, 64), F32)]
-                            across.append(jnp.concatenate(([jnp.zeros((2, 64), F32)] if ew else []) + down, axis=0))
+                            down = [w_down1[kh, ch].astype(F32), jnp.zeros((4 - 2 * ew, HALF), F32)]
+                            across.append(jnp.concatenate(([jnp.zeros((2, HALF), F32)] if ew else []) + down, axis=0))
                         else:
-                            across.append(jnp.zeros((8, 64), F32))
+                            across.append(jnp.zeros((8, HALF), F32))
                 blocks.append(jnp.concatenate(across, axis=1))
         blocks.append(jnp.zeros((32, C), F32))
         wd1[L * dh:L * dh + L, :] = jnp.concatenate(blocks, axis=0).astype(BF16)
+
+
+def pack_conv1(w_conv1, wc1):
     for dw in range(2):
         for mw in range(2):
             for dh in range(2):
@@ -397,18 +433,21 @@
                         for ew in range(2):
                             kh, kw = 2 * dh + mh - eh, 2 * dw + mw - ew
                             inside = 0 <= kh < 3 and 0 <= kw < 3
-                            across.append(w_conv1[kh, kw] if inside else jnp.zeros((64, 64), BF16))
-                    at = (2 * mh + mw) * 64
-                    wc1[dw, dh, at:at + 64, :] = jnp.concatenate(across, axis=1)
+                            across.append(w_conv1[kh, kw] if inside else jnp.zeros((HALF, HALF), BF16))
+                    at = (2 * mh + mw) * HALF
+                    wc1[dw, dh, at:at + HALF, :] = jnp.concatenate(across, axis=1)
+
+
+def pack_stage2(w_down2, w_conv2, wd2, wc2):
     for dw in range(3):
         for mw in range(2):
             for dh in range(2):
                 for mh in range(2):
-                    at = (2 * mh + mw) * 64
+                    at = (2 * mh + mw) * HALF
                     for ew in range(2):
                         kw = 2 * dw + mw - 2 * ew
-                        value = w_down2[2 * dh + mh, kw] if 0 <= kw < 4 else jnp.zeros((64, L), BF16)
-                        wd2[dw, dh, at:at + 64, L * ew:L * ew + L] = value
+                        value = w_down2[2 * dh + mh, kw] if 0 <= kw < 4 else jnp.zeros((HALF, L), BF16)
+                        wd2[dw, dh, at:at + HALF, L * ew:L * ew + L] = value
     for dw in range(2):
         for mw in range(2):
             for kh in range(3):
@@ -443,9 +482,9 @@
             in_specs=[hbm, vmem, vmem] + [hbm, vmem] * 5,
             out_specs=hbm,
             scratch_shapes=[pltpu.VMEM((N, 3, L, L), BF16)] + weight_in + [pltpu.VMEM((N, 3, 8, L), BF16)] * 2
-            + [pltpu.VMEM((3, 17 * (L + N), L), F32), pltpu.VMEM((12, 144, PIX), F32)] + [strip] * 4
+            + [pltpu.VMEM((3, PITCH * (L + N), L), F32), pltpu.VMEM((12, 144, PIX), F32), pltpu.VMEM((34, 2, N, L), BF16)] + [strip] * 4
             + [act(34, 34), act(33, 33), act(18, 36), act(17, 34), act(18, 18)] + weights
-            + [pltpu.VMEM((8, C), F32), pltpu.VMEM((6, 2, 17 * N, L), F32), act(N, N), dma((28,)), dma((28,)), dma((6,)), dma((4,))],
+            + [pltpu.VMEM((8, C), F32), pltpu.VMEM((6, 2, PITCH * N, L), F32), act(N, N), dma((28,)), dma((28,)), dma((6,)), dma((5,))],
             compiler_params=pltpu.CompilerParams(collective_id=0, has_side_effects=True, vmem_limit_bytes=66_000_000),
             name='encoder',
         )(x, jnp.transpose(w_down1, (0, 2, 1, 3)), row(b_down1), w_conv1, row(b_conv1), w_down2, row(b_down2), w_conv2, row(b_conv2),

time: 52.8 us -> 51.1 us (0.968)
  Pallas kernels: 52.4 us -> 50.8 us
    pallas_call x1, Pallas kernels: 50 us -> 48.4 us  [local(): pl.pallas_call(functools.partial(body, rows, cols), out_shape=jax.ShapeDt...]
where the time goes in v5:
time: 51.1 us; the launch traced here: 51 us
  Pallas kernels  50.8 us (99%)
    pallas_call x1, Pallas kernels, local(): pl.pallas_call(functools.partial(body, rows, cols), out_shape=jax.ShapeDt...  48.4 us
    pallas_call x1, Pallas kernels, local(): pl.pallas_call(hand_on, out_shape=jax.ShapeDtypeStruct(out.shape, BF16),...  2.39 us

profile of v5, /device:TPU:1, one launch (start us, length us, event | category | flops | bytes accessed | tf_op | source)
XLA Modules:
  0.0 51.0 jit_solution(1350908218576867517)
XLA Ops:
  0.0 48.4 %encoder.1.src = bf16[16,16,16,256]{3,2,1,0:T(8,128)(2,1)} custom-call(bf16[16,3,128,128]{3,2,1,0:T(8,128)(2,1)} %bitcast.8, bf16[4,3,4,64]{3,2,1,0:T(4,128)(2,1)} %bitcast.9, f32[1,64]{1,0:T(1,128)} %bitcast.12, bf16[3,3,64,64]{3,2,1,0:T(8,128)(2,1)} %w_conv1_hbm.1, f32[1,64]{1,0:T(1,128)} %bitcast.13, bf16[4,4,64,128]{3,2,1,0:T(8,128)(2,1)} %w_down2_hbm.1, ...), custom_call_target="tpu_custom_call" | custom-call | tf_op jit(solution)/shard_map/encoder/pallas_call | solution.py:479
  48.4 2.4 %hand_on.1 = bf16[16,16,16,256]{3,2,1,0:T(8,128)(2,1)} custom-call(bf16[16,16,16,256]{3,2,1,0:T(8,128)(2,1)} %encoder.1.src), custom_call_target="tpu_custom_call" | custom-call | tf_op jit(solution)/shard_map/hand_on/pallas_call | solution.py:492

commit v6 on v5

--- a/solution.py
+++ b/solution.py
@@ -74,6 +74,8 @@
     def _():
         to_up.start()
 
+    up, dn, lf, rt = (jnp.where(there, jnp.inf, 0.0).astype(F32) for there in (has_up, has_dn, has_lf, has_rt))
+
     def clear(ref, there, index):
         @pl.when(jnp.logical_not(there))
         def _():
@@ -82,6 +84,13 @@
     every = slice(None)
     clear(top, has_up, (every,))
     clear(bot, has_dn, (every,))
+    clear(recv_l, has_lf, (every,))
+    clear(recv_r, has_rt, (every,))
+    for ref, step, last in ((y2, 2, 34), (y3, 1, N + 1)):
+        clear(ref, has_up, (every, slice(0, step)))
+        clear(ref, has_dn, (every, slice(last, last + step)))
+        clear(ref, has_lf, (slice(0, 1),))
+        clear(ref, has_rt, (slice(N + 1, N + 2),))
     pack_down1(w_down1, wd1)
     for k, b in enumerate((b_down1, b_conv1, b_down2, b_conv2, b_down3, b_conv3)):
         biases[k:k + 1, :] = jnp.concatenate([b[...]] * (C // b.shape[1]), axis=1)
@@ -118,8 +127,21 @@
             acc = d if acc is None else acc + d
         return acc
 
+    def relu(acc, k, shape):
+        return jnp.maximum(acc + biases[k:k + 1, :], 0.0).reshape(shape)
+
     def finish(acc, k, shape):
-        return jnp.maximum(acc + biases[k:k + 1, :], 0.0).astype(BF16).reshape(shape)
+        return relu(acc, k, shape).astype(BF16)
+
+    def bound(v, inside, first=0, last=C):
+        parts = [v[..., :first], jnp.minimum(v[..., first:last], inside), v[..., last:]]
+        return jnp.concatenate([p for p in parts if p.shape[-1]], axis=-1)
+
+    def put_rows(ref, w, v, first=(0, C), last=(0, C)):
+        h = v.shape[0]
+        ref[w, 0:1] = bound(v[0:1], up, *first).astype(BF16)
+        ref[w, 1:h - 1] = v[1:h - 1].astype(BF16)
+        ref[w, h - 1:h] = bound(v[h - 1:h], dn, *last).astype(BF16)
 
     def window(k, e, lanes):
         size = sum(last - first for first, last in lanes)
@@ -132,7 +154,10 @@
         for e in range(2):
             xb = window(k, e, [(0, PIX)])
             lhs = jnp.concatenate([xb[0:m], xb[N:N + m]], axis=1)
-            y1[2 * k + e] = finish(dots([(lhs, wd1[...])]), 0, (34, N, C))
+            v = relu(dots([(lhs, wd1[...])]), 0, (34, N, C))
+            if 2 * k + e in (0, 33):
+                v = jnp.minimum(v, rt if k else lf)
+            put_rows(y1, 2 * k + e, v)
 
     def down1_inner(k):
         m = 23 * N
@@ -150,9 +175,12 @@
             this = jnp.concatenate([xb[0:L], kept[2 * k + e, 1], xb[L:L + 2 * N]], axis=0)
             below = jnp.concatenate([xb[N:L], kept[2 * k + e, 0], xb[L:L + 3 * N]], axis=0)
             lhs.append(jnp.concatenate([this, below], axis=1))
-        res = finish(dots([(jnp.concatenate(lhs, axis=0), wd1[...])]), 0, (2, 11, N, C))
-        y1[2 * k:2 * k + 2, 0:8] = res[:, 0:8]
-        y1[2 * k:2 * k + 2, 31:34] = res[:, 8:11]
+        v = relu(dots([(jnp.concatenate(lhs, axis=0), wd1[...])]), 0, (2, 11, N, C))
+        both = slice(2 * k, 2 * k + 2)
+        y1[both, 0:1] = bound(v[:, 0:1], up).astype(BF16)
+        y1[both, 1:8] = v[:, 1:8].astype(BF16)
+        y1[both, 31:33] = v[:, 8:10].astype(BF16)
+        y1[both, 33:34] = bound(v[:, 10:11], dn).astype(BF16)
 
     for k in range(1, N):
         down1_inner(k)
@@ -199,16 +227,21 @@
 
     def conv1(b):
         pairs = [(y1[b + dw, dh:dh + 33].reshape(33 * N, C), wc1[dw, dh]) for dw in range(2) for dh in range(2)]
-        z1[b] = finish(dots(pairs), 1, (33, N, C))
+        v = relu(dots(pairs), 1, (33, N, C))
+        if isinstance(b, int):
+            for half in (0, L):
+                if b == 0:
+                    v = bound(v, lf, half, half + HALF)
+                if b == 32:
+                    v = bound(v, rt, half + HALF, half + L)
+        put_rows(z1, b, v, (0, L), (L, C))
 
     for copy in loads[1:4]:
         copy.wait()
     pack_conv1(w_conv1, wc1)
     for k in range(1, N):
         down1_outer(k)
-    clear(y1, has_up, (slice(2, 32), slice(0, 1)))
-    clear(y1, has_dn, (slice(2, 32), slice(33, 34)))
-    loop(2, 30, 14, conv1)
+    loop(2, 18, 16, conv1)
 
     @pl.when(has_lf)
     def _():
@@ -220,25 +253,13 @@
         to_rt.wait_send()
         to_lf.wait_recv()
 
-    clear(recv_l, has_lf, (every,))
-    clear(recv_r, has_rt, (every,))
     tt[:, 0:5, :] = recv_l[...].astype(F32)[:, 3:8]
     tt[:, 5 + L:13 + L, :] = recv_r[...].astype(F32)
     down1(0)
     down1(N)
-    for part in (slice(0, 2), slice(32, 34)):
-        clear(y1, has_up, (part, slice(0, 1)))
-        clear(y1, has_dn, (part, slice(33, 34)))
-    clear(y1, has_lf, (slice(0, 1),))
-    clear(y1, has_rt, (slice(33, 34),))
     pack_stage2(w_down2, w_conv2, wd2, wc2)
-    for b in (0, 1, 30, 31, 32):
+    for b in (*range(18, 33), 0, 1):
         conv1(b)
-    clear(z1, has_up, (every, slice(0, 1), every, slice(0, L)))
-    clear(z1, has_dn, (every, slice(32, 33), every, slice(L, C)))
-    for half in (0, L):
-        clear(z1, has_lf, (slice(0, 1), every, every, slice(half, half + HALF)))
-        clear(z1, has_rt, (slice(32, 33), every, every, slice(half + HALF, half + L)))
 
     def edge(d, around, size, step):
         first, last = around, around + size
@@ -286,7 +307,12 @@
 
     def conv2(q):
         pairs = [(y2[q + dw, dh:dh + 34].reshape(34 * N, C), wc2[dw, dh]) for dw in range(2) for dh in range(3)]
-        z2[q] = finish(dots(pairs), 3, (34, N, C))
+        v = relu(dots(pairs), 3, (34, N, C))
+        if q == 0:
+            v = bound(v, lf, 0, L)
+        if q == N:
+            v = bound(v, rt, L, C)
+        put_rows(z2, q, v)
 
     def conv2_inner(q):
         pairs = [(y2[q + dw, dh + 2:dh + 32].reshape(30 * N, C), wc2[dw, dh]) for dw in range(2) for dh in range(3)]
@@ -298,15 +324,12 @@
             for dh in range(3):
                 lhs = [y2[q + dw, h + dh:h + dh + 2].reshape(2 * N, C) for q in range(first, last) for h in (0, 32)]
                 pairs.append((jnp.concatenate(lhs, axis=0), wc2[dw, dh]))
-        res = finish(dots(pairs), 3, (last - first, 4, N, C))
-        z2[first:last, 0:2] = res[:, 0:2]
-        z2[first:last, 32:34] = res[:, 2:4]
-
-    for ref, step, last in ((y2, 2, 34), (y3, 1, 17)):
-        clear(ref, has_up, (every, slice(0, step)))
-        clear(ref, has_dn, (every, slice(last, last + step)))
-        clear(ref, has_lf, (slice(0, 1),))
-        clear(ref, has_rt, (slice(17, 18),))
+        v = relu(dots(pairs), 3, (last - first, 4, N, C))
+        z2[first:last, 0:1] = bound(v[:, 0:1], up).astype(BF16)
+        z2[first:last, 1:2] = v[:, 1:2].astype(BF16)
+        z2[first:last, 32:33] = v[:, 2:3].astype(BF16)
+        z2[first:last, 33:34] = bound(v[:, 3:4], dn).astype(BF16)
+
     down2(0)
     down2(N - 1)
     start(y2_cols)
@@ -318,15 +341,8 @@
         conv2_inner(q)
     for copies in (*y2_rows, y2_cols):
         finished(copies)
-    outer_q = (slice(0, 3), slice(14, 17))
-    for part in outer_q:
-        for q in range(part.start, part.stop):
-            conv2(q)
-    for part in outer_q:
-        clear(z2, has_up, (part, slice(0, 1)))
-        clear(z2, has_dn, (part, slice(33, 34)))
-    clear(z2, has_lf, (slice(0, 1), every, every, slice(0, L)))
-    clear(z2, has_rt, (slice(N, N + 1), every, every, slice(L, C)))
+    for q in (0, 1, 2, 14, 15, N):
+        conv2(q)
     for copy in loads[4:]:
         copy.wait()
 
@@ -344,8 +360,6 @@
     conv2_inner(12)
     conv2_inner(13)
     conv2_rest(3, 14)
-    clear(z2, has_up, (slice(3, 14), slice(0, 1)))
-    clear(z2, has_dn, (slice(3, 14), slice(33, 34)))
     for k in range(1, 7):
         down3(k)
     start(y3_rows)

time: 51.1 us -> 50 us (0.978)
  Pallas kernels: 50.8 us -> 49.6 us
    pallas_call x1, Pallas kernels: 48.4 us -> 47.2 us  [local(): pl.pallas_call(functools.partial(body, rows, cols), out_shape=jax.ShapeDt...]
where the time goes in v6:
time: 50 us; the launch traced here: 49.8 us
  Pallas kernels  49.6 us (99%)
    pallas_call x1, Pallas kernels, local(): pl.pallas_call(functools.partial(body, rows, cols), out_shape=jax.ShapeDt...  47.2 us
    pallas_call x1, Pallas kernels, local(): pl.pallas_call(hand_on, out_shape=jax.ShapeDtypeStruct(out.shape, BF16),...  2.39 us

profile of v6, /device:TPU:1, one launch (start us, length us, event | category | flops | bytes accessed | tf_op | source)
XLA Modules:
  0.0 49.8 jit_solution(9534543008345401659)
XLA Ops:
  0.0 47.2 %encoder.1.src = bf16[16,16,16,256]{3,2,1,0:T(8,128)(2,1)} custom-call(bf16[16,3,128,128]{3,2,1,0:T(8,128)(2,1)} %bitcast.8, bf16[4,3,4,64]{3,2,1,0:T(4,128)(2,1)} %bitcast.9, f32[1,64]{1,0:T(1,128)} %bitcast.12, bf16[3,3,64,64]{3,2,1,0:T(8,128)(2,1)} %w_conv1_hbm.1, f32[1,64]{1,0:T(1,128)} %bitcast.13, bf16[4,4,64,128]{3,2,1,0:T(8,128)(2,1)} %w_down2_hbm.1, ...), custom_call_target="tpu_custom_call" | custom-call | tf_op jit(solution)/shard_map/encoder/pallas_call | solution.py:493
  47.2 2.4 %hand_on.1 = bf16[16,16,16,256]{3,2,1,0:T(8,128)(2,1)} custom-call(bf16[16,16,16,256]{3,2,1,0:T(8,128)(2,1)} %encoder.1.src), custom_call_target="tpu_custom_call" | custom-call | tf_op jit(solution)/shard_map/hand_on/pallas_call | solution.py:506

commit v7 on v6

--- a/solution.py
+++ b/solution.py
@@ -19,16 +19,18 @@
 PITCH = 17
 
 
-def body(rows, cols, x_hbm, w_down1, b_down1, w_conv1_hbm, b_conv1, w_down2_hbm, b_down2, w_conv2_hbm, b_conv2, w_down3, b_down3,
-         w_conv3, b_conv3, out_hbm, x_ref, w_conv1, w_down2, w_conv2, top, bot, xs, tt, kept, send_l, send_r, recv_l, recv_r, y1, z1, y2, z2, y3,
-         wd1, wc1, wd2, wc2, wd3, wc3, biases, turn, out_ref, ssem, rsem, wsem, osem):
+def body(rows, cols, x_hbm, w_down1_hbm, w_conv1_hbm, w_down2_hbm, w_conv2_hbm, w_down3, w_conv3, *refs):
+    b_hbm, out_hbm, bs = refs[:6], refs[6], refs[7:13]
+    (x_ref, w_down1, w_conv1, w_down2, w_conv2, top, bot, xs, tt, kept, send_l, send_r, recv_l, recv_r, y1, z1, y2, z2,
+     y3, wd1, wc1, wd2, wc2, wd3, wc3, biases, turn, out_ref, ssem, rsem, wsem, osem) = refs[13:]
     r = lax.axis_index('row')
     c = lax.axis_index('col')
     has_up, has_dn = r > 0, r < rows - 1
     has_lf, has_rt = c > 0, c < cols - 1
 
     loads = [pltpu.make_async_copy(src, dst, wsem.at[k]) for k, (src, dst) in enumerate((
-        (x_hbm, x_ref), (w_conv1_hbm, w_conv1), (w_down2_hbm, w_down2), (w_conv2_hbm, w_conv2), (w_down3, wd3), (w_conv3, wc3)))]
+        (x_hbm, x_ref), (w_conv1_hbm, w_conv1), (w_down2_hbm, w_down2), (w_conv2_hbm, w_conv2), (w_down3, wd3), (w_conv3, wc3),
+        (w_down1_hbm, w_down1), *zip(b_hbm, bs)))]
     for copy in loads:
         copy.start()
 
@@ -91,8 +93,10 @@
         clear(ref, has_dn, (every, slice(last, last + step)))
         clear(ref, has_lf, (slice(0, 1),))
         clear(ref, has_rt, (slice(N + 1, N + 2),))
+    for copy in loads[6:]:
+        copy.wait()
     pack_down1(w_down1, wd1)
-    for k, b in enumerate((b_down1, b_conv1, b_down2, b_conv2, b_down3, b_conv3)):
+    for k, b in enumerate(bs):
         biases[k:k + 1, :] = jnp.concatenate([b[...]] * (C // b.shape[1]), axis=1)
 
     def gather(ch, src, h, size):
@@ -343,7 +347,7 @@
         finished(copies)
     for q in (0, 1, 2, 14, 15, N):
         conv2(q)
-    for copy in loads[4:]:
+    for copy in loads[4:6]:
         copy.wait()
 
     def down3(k):
@@ -398,9 +402,10 @@
     last = [put_out(13, 2, 2), put_out(0, 1, 3), put_out(15, 1, 4)]
     conv3((13, 14), 0)
     last[0].start()
-    conv3((0, 15), 1)
-    for copy in last[1:]:
-        copy.start()
+    conv3((0,), 1)
+    last[1].start()
+    conv3((15,), 2)
+    last[2].start()
     for copy in (put_out(1, 6, 0), put_out(7, 6, 1), *last):
         copy.wait()
 
@@ -477,32 +482,29 @@
     def local(images, w_down1, b_down1, w_conv1, b_conv1, w_down2, b_down2, w_conv2, b_conv2, w_down3, b_down3, w_conv3, b_conv3):
         x = jnp.transpose(images, (0, 3, 1, 2))
 
-        def row(b):
-            return b.reshape(1, -1)
-
         def act(w, h):
             return pltpu.VMEM((w, h, N, C), BF16)
 
-        vmem = pl.BlockSpec(memory_space=pltpu.VMEM)
         hbm = pl.BlockSpec(memory_space=pl.ANY)
         strip = pltpu.VMEM((12, 8, PIX), BF16)
-        weight_in = [pltpu.VMEM(w.shape, BF16) for w in (w_conv1, w_down2, w_conv2)]
+        taps1 = jnp.transpose(w_down1, (0, 2, 1, 3))
+        bias_rows = [b.reshape(1, -1) for b in (b_down1, b_conv1, b_down2, b_conv2, b_down3, b_conv3)]
+        weight_in = [pltpu.VMEM(w.shape, BF16) for w in (taps1, w_conv1, w_down2, w_conv2)]
         weights = [pltpu.VMEM(shape, BF16) for shape in
                    ((C, C), (2, 2, C, C), (3, 2, C, C), (2, 3, C, C), w_down3.shape, w_conv3.shape)]
         dma = pltpu.SemaphoreType.DMA
         out = pl.pallas_call(
             functools.partial(body, rows, cols),
             out_shape=jax.ShapeDtypeStruct((N, N, N, C), BF16),
-            in_specs=[hbm, vmem, vmem] + [hbm, vmem] * 5,
+            in_specs=[hbm] * 13,
             out_specs=hbm,
-            scratch_shapes=[pltpu.VMEM((N, 3, L, L), BF16)] + weight_in + [pltpu.VMEM((N, 3, 8, L), BF16)] * 2
+            scratch_shapes=[pltpu.VMEM(b.shape, F32) for b in bias_rows] + [pltpu.VMEM((N, 3, L, L), BF16)] + weight_in + [pltpu.VMEM((N, 3, 8, L), BF16)] * 2
             + [pltpu.VMEM((3, PITCH * (L + N), L), F32), pltpu.VMEM((12, 144, PIX), F32), pltpu.VMEM((34, 2, N, L), BF16)] + [strip] * 4
             + [act(34, 34), act(33, 33), act(18, 36), act(17, 34), act(18, 18)] + weights
-            + [pltpu.VMEM((8, C), F32), pltpu.VMEM((6, 2, PITCH * N, L), F32), act(N, N), dma((28,)), dma((28,)), dma((6,)), dma((5,))],
+            + [pltpu.VMEM((8, C), F32), pltpu.VMEM((6, 2, PITCH * N, L), F32), act(N, N), dma((28,)), dma((28,)), dma((13,)), dma((5,))],
             compiler_params=pltpu.CompilerParams(collective_id=0, has_side_effects=True, vmem_limit_bytes=66_000_000),
             name='encoder',
-        )(x, jnp.transpose(w_down1, (0, 2, 1, 3)), row(b_down1), w_conv1, row(b_conv1), w_down2, row(b_down2), w_conv2, row(b_conv2),
-          w_down3, row(b_down3), w_conv3, row(b_conv3))
+        )(x, taps1, w_conv1, w_down2, w_conv2, w_down3, w_conv3, *bias_rows)
         return pl.pallas_call(
             hand_on,
             out_shape=jax.ShapeDtypeStruct(out.shape, BF16),

time: 50 us -> 49.3 us (0.986)
  Pallas kernels: 49.6 us -> 48.9 us
    pallas_call x1, Pallas kernels: 47.2 us -> 46.5 us  [local(): pl.pallas_call(functools.partial(body, rows, cols), out_shape=jax.ShapeDt...]
where the time goes in v7:
time: 49.3 us; the launch traced here: 49.1 us
  Pallas kernels  48.9 us (99%)
    pallas_call x1, Pallas kernels, local(): pl.pallas_call(functools.partial(body, rows, cols), out_shape=jax.ShapeDt...  46.5 us
    pallas_call x1, Pallas kernels, local(): pl.pallas_call(hand_on, out_shape=jax.ShapeDtypeStruct(out.shape, BF16),...  2.39 us

profile of v7, /device:TPU:1, one launch (start us, length us, event | category | flops | bytes accessed | tf_op | source)
XLA Modules:
  0.0 49.1 jit_solution(12483607174403481362)
XLA Ops:
  0.0 46.5 %encoder.1.src = bf16[16,16,16,256]{3,2,1,0:T(8,128)(2,1)} custom-call(bf16[16,3,128,128]{3,2,1,0:T(8,128)(2,1)} %bitcast.8, bf16[4,3,4,64]{3,2,1,0:T(4,128)(2,1)} %bitcast.9, bf16[3,3,64,64]{3,2,1,0:T(8,128)(2,1)} %w_conv1_hbm.1, bf16[4,4,64,128]{3,2,1,0:T(8,128)(2,1)} %w_down2_hbm.1, bf16[3,3,128,128]{3,2,1,0:T(8,128)(2,1)} %w_conv2_hbm.1, ...), custom_call_target="tpu_custom_call" | custom-call | tf_op jit(solution)/shard_map/encoder/pallas_call | solution.py:496
  46.6 2.4 %hand_on.1 = bf16[16,16,16,256]{3,2,1,0:T(8,128)(2,1)} custom-call(bf16[16,16,16,256]{3,2,1,0:T(8,128)(2,1)} %encoder.1.src), custom_call_target="tpu_custom_call" | custom-call | tf_op jit(solution)/shard_map/hand_on/pallas_call | solution.py:508

commit v8 on v7

--- a/solution.py
+++ b/solution.py
@@ -31,8 +31,6 @@
     loads = [pltpu.make_async_copy(src, dst, wsem.at[k]) for k, (src, dst) in enumerate((
         (x_hbm, x_ref), (w_conv1_hbm, w_conv1), (w_down2_hbm, w_down2), (w_conv2_hbm, w_conv2), (w_down3, wd3), (w_conv3, wc3),
         (w_down1_hbm, w_down1), *zip(b_hbm, bs)))]
-    for copy in loads:
-        copy.start()
 
     neighbours = []
     for dr in (-1, 0, 1):
@@ -58,6 +56,8 @@
         @pl.when(there)
         def _():
             pl.semaphore_signal(barrier, inc=1, device_id=device(dr, dc), device_id_type=MESH)
+    for copy in loads:
+        copy.start()
     pl.semaphore_wait(barrier, sum(t.astype(jnp.int32) for t in (has_up, has_dn, has_lf, has_rt)))
 
     def remote(src, dst, k, dr, dc):
@@ -411,7 +411,7 @@
 
 
 def hand_on(src, dst, held, isem, osem):
-    parts = [pl.ds(2 * k, 2) for k in range(8)]
+    parts = [pl.ds(k, 1) for k in range(N)]
     reads = [pltpu.make_async_copy(src.at[p], held.at[p], isem.at[k]) for k, p in enumerate(parts)]
     writes = [pltpu.make_async_copy(held.at[p], dst.at[p], osem.at[k]) for k, p in enumerate(parts)]
     for copy in reads:
@@ -510,7 +510,7 @@
             out_shape=jax.ShapeDtypeStruct(out.shape, BF16),
             in_specs=[hbm],
             out_specs=hbm,
-            scratch_shapes=[act(N, N), dma((8,)), dma((8,))],
+            scratch_shapes=[act(N, N), dma((N,)), dma((N,))],
             name='hand_on',
         )(out)
 

time: 49.3 us -> 49.6 us (level)
  no operation moved by 1% of the time
where the time goes in v8:
time: 49.6 us; the launch traced here: 49.3 us
  Pallas kernels  49.1 us (99%)
    pallas_call x1, Pallas kernels, local(): pl.pallas_call(functools.partial(body, rows, cols), out_shape=jax.ShapeDt...  46.5 us
    pallas_call x1, Pallas kernels, local(): pl.pallas_call(hand_on, out_shape=jax.ShapeDtypeStruct(out.shape, BF16),...  2.57 us

profile of v8, /device:TPU:1, one launch (start us, length us, event | category | flops | bytes accessed | tf_op | source)
XLA Modules:
  0.0 49.3 jit_solution(16876829215062434718)
XLA Ops:
  0.0 46.5 %encoder.1.src = bf16[16,16,16,256]{3,2,1,0:T(8,128)(2,1)} custom-call(bf16[16,3,128,128]{3,2,1,0:T(8,128)(2,1)} %bitcast.8, bf16[4,3,4,64]{3,2,1,0:T(4,128)(2,1)} %bitcast.9, bf16[3,3,64,64]{3,2,1,0:T(8,128)(2,1)} %w_conv1_hbm.1, bf16[4,4,64,128]{3,2,1,0:T(8,128)(2,1)} %w_down2_hbm.1, bf16[3,3,128,128]{3,2,1,0:T(8,128)(2,1)} %w_conv2_hbm.1, ...), custom_call_target="tpu_custom_call" | custom-call | tf_op jit(solution)/shard_map/encoder/pallas_call | solution.py:496
  46.5 2.6 %hand_on.1 = bf16[16,16,16,256]{3,2,1,0:T(8,128)(2,1)} custom-call(bf16[16,16,16,256]{3,2,1,0:T(8,128)(2,1)} %encoder.1.src), custom_call_target="tpu_custom_call" | custom-call | tf_op jit(solution)/shard_map/hand_on/pallas_call | solution.py:508
